TPU v7x, 256 devices: a whole 4x4x8 slice. The times are simulated.
256 devices in a mesh: cls: 8 (over x, y_hi), str: 32 (over z, y_lo, core).
Axes of the slice: x: 4, y: 4 (y_hi: 2, y_lo: 2; y = y_hi * 2 + y_lo), z: 8, core: 2. Of those that a mesh axis runs over, the one named last changes fastest.
Arguments:
- first_factor_tiles: float32 [8, 1024, 2, 4, 1024], P(None, ('cls', 'str')), may hold values from -6 to 6
- b_blocks: float32 [8, 1024, 2, 4, 512], P(None, ('cls', 'str')), may hold values from -0.0625 to 0.0625
Outputs:
- c_blocks: float32 [8, 1024, 2, 4, 512], P(None, ('cls', 'str'))
All inputs are finite; a program needn't handle non-finite values.
Results may differ from a plain program's by a relative error of at most 0.0003.
Values sent between devices are 32-bit elements; how exact they have to be, the bound alone decides.
No kernel may reach another device: no remote copies, remote signals or barrier semaphores. Data moves between devices by JAX's collectives and lax.ppermute only.
A program may use at most 64 MiB of HBM per device.

v0:
```python
import jax
import jax.numpy as jnp
from jax import lax
from jax.experimental import pallas as pl
from jax.experimental.pallas import tpu as pltpu
from jax.sharding import Mesh
from jax.sharding import PartitionSpec as P

AXES = ("x", "yh", "z", "yl", "c")
Y = ("yh", "yl")
F32, BF16 = jnp.float32, jnp.bfloat16


def swap(v, axis, bits):
    n = lax.axis_size(axis)
    return lax.ppermute(v, axis, [(i, i ^ bits) for i in range(n)])


def shift(v, axis, step):
    n = lax.axis_size(axis)
    return lax.ppermute(v, axis, [(i, (i + step) % n) for i in range(n)])


def pick(pieces, index):
    low = jnp.where(index % 2 == 1, pieces[1], pieces[0])
    high = jnp.where(index % 2 == 1, pieces[3], pieces[2])
    return jnp.where(index >= 2, high, low)


def lane_order(z, c):
    src = lax.broadcasted_iota(jnp.int32, (256, 256), 0)
    dst = lax.broadcasted_iota(jnp.int32, (256, 256), 1)
    yh, zz, yl, cc, q = src // 128, (src // 16) % 8, (src // 8) % 2, (src // 4) % 2, src % 4
    to = ((cc ^ c) * 128) + ((zz - z) % 8) * 16 + yh * 8 + yl * 4 + q
    return (to == dst).astype(F32)


def parts(v):
    high = v.astype(BF16)
    return high, (v - high.astype(F32)).astype(BF16)


def split_left(left):
    n = len(left)

    def kernel(*refs):
        high_ref, low_ref = refs[n:]

        def step(b, carry):
            at = pl.ds(pl.multiple_of(b * 256, 256), 256)
            for g in range(n):
                for d in range(2):
                    rows = pl.ds(64 * g + 32 * d, 32)
                    high_ref[rows, at], low_ref[rows, at] = parts(refs[g][d, b])
            return carry

        lax.fori_loop(0, 8, step, 0)

    return pl.pallas_call(
        kernel,
        out_shape=(jax.ShapeDtypeStruct((64 * n, 2048), BF16),) * 2,
        in_specs=[pl.BlockSpec(memory_space=pltpu.VMEM)] * n,
        out_specs=(pl.BlockSpec(memory_space=pltpu.VMEM),) * 2,
        compiler_params=pltpu.CompilerParams(vmem_limit_bytes=40 * 1024 * 1024),
        name="split_left",
    )(*left)


def product(left, right):
    arrays = []
    for v, _ in right:
        if not any(v is w for w in arrays):
            arrays.append(v)
    where = [(next(k for k, w in enumerate(arrays) if w is v), i) for v, i in right]
    n = len(arrays)

    def kernel(ah, al, *refs):
        o_ref, bh, bl = refs[n:]

        def split(b, carry):
            for k, (r, i) in enumerate(where):
                at = pl.ds(pl.multiple_of(b * 256 + k * 16, 16), 16)
                bh[at, :], bl[at, :] = parts(refs[r][i, b])
            return carry

        lax.fori_loop(0, 8, split, 0)

        def rows(m, carry):
            at = pl.ds(pl.multiple_of(m * 128, 128), 128)
            total = jnp.dot(ah[at, :], bh[...], preferred_element_type=F32)
            total += jnp.dot(ah[at, :], bl[...], preferred_element_type=F32)
            total += jnp.dot(al[at, :], bh[...], preferred_element_type=F32)
            o_ref[at, :] = total
            return carry

        lax.fori_loop(0, 4, rows, 0)

    return pl.pallas_call(
        kernel,
        out_shape=jax.ShapeDtypeStruct((512, 512), F32),
        in_specs=[pl.BlockSpec(memory_space=pltpu.VMEM)] * (n + 2),
        out_specs=pl.BlockSpec(memory_space=pltpu.VMEM),
        scratch_shapes=[pltpu.VMEM((2048, 512), BF16)] * 2,
        compiler_params=pltpu.CompilerParams(vmem_limit_bytes=40 * 1024 * 1024),
        name="product",
    )(*left, *arrays)


def placed_product(a, b):
    x, z, c = lax.axis_index("x"), lax.axis_index("z"), lax.axis_index("c")
    y = lax.axis_index(Y)

    bg = b.reshape(8, 4, 4, 1024)
    b_for = [lax.dynamic_index_in_dim(bg, y ^ d, axis=2, keepdims=False) for d in range(4)]
    b_got = [b_for[0]] + [swap(b_for[d], Y, d) for d in (1, 2, 3)]
    block = jnp.stack([pick(b_got, y ^ k) for k in range(4)], axis=1).reshape(8, 16, 1024)
    halves = [block[:, :, :512], block[:, :, 512:]]

    ordered = jnp.dot(a.reshape(32, 8, 4, 256), lane_order(z, c), precision=lax.Precision.HIGHEST)
    ordered = jnp.transpose(ordered, (2, 1, 0, 3))
    a_for = [lax.dynamic_index_in_dim(ordered, x ^ d, axis=0, keepdims=False) for d in range(4)]
    a_got = [a_for[0]] + [swap(a_for[d], "x", d) for d in (1, 2, 3)]
    low, high = jnp.stack(a_got[:2]), jnp.stack(a_got[2:])
    near3_low, near1_high = swap(low, Y, 3), swap(high, Y, 1)
    near1_low, near3_high = swap(low, Y, 1), swap(high, Y, 3)
    far_low, far_high = swap(near3_low, Y, 1), swap(near1_high, Y, 3)
    left = split_left([low, high, near1_low, near1_high, far_low, far_high, near3_low, near3_high])

    own, other = [{}, {}], [{}, {}]
    both = jnp.stack(halves)
    crossed = swap(both, "c", 1)
    up, down = list(halves), list(halves)
    for h in range(2):
        own[h][0], other[h][0] = (both, h), (crossed, h)
    for s in (1, 2, 3):
        for h in range(2):
            up[h] = shift(up[h], "z", 1)
            down[h] = shift(down[h], "z", -1)
        both = jnp.stack([up[0], down[0], up[1], down[1]])
        crossed = swap(both, "c", 1)
        for h in range(2):
            for i, at in ((2 * h, 8 - s), (2 * h + 1, s)):
                own[h][at], other[h][at] = (both, i), (crossed, i)
    last = [shift(up[0], "z", 1), shift(down[1], "z", -1)]
    for h in range(2):
        crossed = swap(last[h], "c", 1)
        own[h][4], other[h][4] = (last[h][None], 0), (crossed[None], 0)
    out = [
        product(left, [own[h][s] for s in range(8)] + [other[h][s] for s in range(8)]).reshape(4, 4, 32, 512)
        for h in range(2)
    ]

    sums = []
    for p, first, second in ((out[0], 1, 3), (out[1], 3, 1)):
        got = swap(jnp.stack([p[:, first], p[:, 2]]), "x", first)
        keep, pass_on = p[:, 0] + got[0], p[:, second] + got[1]
        sums.append(keep + swap(pass_on, "x", second))
    summed = jnp.concatenate(sums, axis=2)
    back = [summed[0]] + [swap(summed[d], Y, d) for d in (1, 2, 3)]
    placed = jnp.stack([pick(back, y ^ k) for k in range(4)], axis=1)
    return placed.reshape(8, 4, 2, 4, 512)


def solution(mesh):
    split = Mesh(mesh.devices.reshape(4, 2, 8, 2, 2), AXES)
    spec = P(None, AXES, None, None, None)
    return jax.shard_map(placed_product, mesh=split, in_specs=(spec, spec), out_specs=spec, check_vma=False)
```

profile of v0, /device:TPU:8, one launch (start us, length us, event | category | flops | bytes accessed | tf_op | source)
XLA Modules:
  0.0 139.4 jit_solution(10008942447831375770)
XLA Ops:
  2.2 2.2 %collective-permute-start.11 = (f32[8,4,1024]{2,1,0:T(4,128)S(1)}, f32[8,4,1024]{2,1,0:T(4,128)S(1)}, u32[]{:S(2)}, u32[]{:S(2)}) collective-permute-start(f32[8,4,1024]{2,1,0:T(4,128)S(1)} %bitcast.186), channel_id=1, source_target_pairs={{0,2},{2,0},{32,34},{34,32},{1,3},{3,1},{33,35},{35,33},{4,6},{6,4... | collective-permute-start | bytes 393224 | tf_op jit(solution)/shard_map/ppermute | solution.py:16
  12.9 5.4 %collective-permute-start.15 = (f32[8,16,512]{2,1,0:T(8,128)S(1)}, f32[8,16,512]{2,1,0:T(8,128)S(1)}, u32[]{:S(2)}, u32[]{:S(2)}) collective-permute-start(f32[8,16,512]{2,1,0:T(8,128)S(1)} %get-tuple-element.28), channel_id=1, source_target_pairs={{0,28},{4,0},{8,4},{12,8},{16,12},{20,16},{24,20},{28,24},{1,29},{... | collective-permute-start | bytes 786440 | tf_op jit(solution)/shard_map/ppermute | solution.py:21
  18.4 3.2 %collective-permute-start.13 = (f32[8,16,512]{2,1,0:T(8,128)S(1)}, f32[8,16,512]{2,1,0:T(8,128)S(1)}, u32[]{:S(2)}, u32[]{:S(2)}) collective-permute-start(f32[8,16,512]{2,1,0:T(8,128)S(1)} %get-tuple-element.25), channel_id=1, source_target_pairs={{0,28},{4,0},{8,4},{12,8},{16,12},{20,16},{24,20},{28,24},{1,29},{... | collective-permute-start | bytes 786440 | tf_op jit(solution)/shard_map/ppermute | solution.py:21
  21.6 2.8 %collective-permute-start.2 = (f32[8,32,256]{2,1,0:T(8,128)S(1)}, f32[8,32,256]{2,1,0:T(8,128)S(1)}, u32[]{:S(2)}, u32[]{:S(2)}) collective-permute-start(f32[8,32,256]{2,1,0:T(8,128)S(1)} %get-tuple-element.18), channel_id=1, source_target_pairs={{0,192},{64,128},{128,64},{192,0},{1,193},{65,129},{129,65},{193,1... | collective-permute-start | bytes 786440 | tf_op jit(solution)/shard_map/ppermute | solution.py:16
  25.1 3.7 %collective-permute-start.19 = (f32[8,16,512]{2,1,0:T(8,128)S(1)}, f32[8,16,512]{2,1,0:T(8,128)S(1)}, u32[]{:S(2)}, u32[]{:S(2)}) collective-permute-start(f32[8,16,512]{2,1,0:T(8,128)S(1)} %collective-permute-done.15), channel_id=1, source_target_pairs={{0,28},{4,0},{8,4},{12,8},{16,12},{20,16},{24,20},{28,24},{1,29},{... | collective-permute-start | bytes 786440 | tf_op jit(solution)/shard_map/ppermute | solution.py:21
  30.7 3.7 %collective-permute-start.17 = (f32[8,16,512]{2,1,0:T(8,128)S(1)}, f32[8,16,512]{2,1,0:T(8,128)S(1)}, u32[]{:S(2)}, u32[]{:S(2)}) collective-permute-start(f32[8,16,512]{2,1,0:T(8,128)S(1)} %collective-permute-done.13), channel_id=1, source_target_pairs={{0,28},{4,0},{8,4},{12,8},{16,12},{20,16},{24,20},{28,24},{1,29},{... | collective-permute-start | bytes 786440 | tf_op jit(solution)/shard_map/ppermute | solution.py:21
  34.4 3.0 %collective-permute-start.1 = (f32[8,32,256]{2,1,0:T(8,128)S(1)}, f32[8,32,256]{2,1,0:T(8,128)S(1)}, u32[]{:S(2)}, u32[]{:S(2)}) collective-permute-start(f32[8,32,256]{2,1,0:T(8,128)S(1)} %get-tuple-element.15), channel_id=1, source_target_pairs={{0,128},{64,192},{128,0},{192,64},{1,129},{65,193},{129,1},{193,65... | collective-permute-start | bytes 786440 | tf_op jit(solution)/shard_map/ppermute | solution.py:16
  37.4 3.2 %collective-permute-start.23 = (f32[8,16,512]{2,1,0:T(8,128)S(1)}, f32[8,16,512]{2,1,0:T(8,128)S(1)}, u32[]{:S(2)}, u32[]{:S(2)}) collective-permute-start(f32[8,16,512]{2,1,0:T(8,128)S(1)} %collective-permute-done.19), channel_id=1, source_target_pairs={{0,28},{4,0},{8,4},{12,8},{16,12},{20,16},{24,20},{28,24},{1,29},{... | collective-permute-start | bytes 786440 | tf_op jit(solution)/shard_map/ppermute | solution.py:21
  41.9 3.7 %collective-permute-start.21 = (f32[8,16,512]{2,1,0:T(8,128)S(1)}, f32[8,16,512]{2,1,0:T(8,128)S(1)}, u32[]{:S(2)}, u32[]{:S(2)}) collective-permute-start(f32[8,16,512]{2,1,0:T(8,128)S(1)} %collective-permute-done.17), channel_id=1, source_target_pairs={{0,28},{4,0},{8,4},{12,8},{16,12},{20,16},{24,20},{28,24},{1,29},{... | collective-permute-start | bytes 786440 | tf_op jit(solution)/shard_map/ppermute | solution.py:21
  52.1 3.7 %collective-permute-done.20 = f32[8,16,512]{2,1,0:T(8,128)S(1)} collective-permute-done((f32[8,16,512]{2,1,0:T(8,128)S(1)}, f32[8,16,512]{2,1,0:T(8,128)S(1)}, u32[]{:S(2)}, u32[]{:S(2)}) %collective-permute-start.20) | collective-permute-done | bytes 262176 | tf_op jit(solution)/shard_map/ppermute | solution.py:21
  57.3 5.1 %collective-permute-done.3.refs_2_ = f32[2,8,32,256]{3,2,1,0:T(8,128)S(1)} collective-permute-done((f32[2,8,32,256]{3,2,1,0:T(8,128)S(1)}, f32[2,8,32,256]{3,2,1,0:T(8,128)S(1)}, u32[]{:S(2)}, u32[]{:S(2)}) %collective-permute-start.3) | collective-permute-done | bytes 524320 | tf_op jit(solution)/shard_map/ppermute | solution.py:16
  62.4 9.2 %collective-permute-done.4.refs_3_ = f32[2,8,32,256]{3,2,1,0:T(8,128)S(1)} collective-permute-done((f32[2,8,32,256]{3,2,1,0:T(8,128)S(1)}, f32[2,8,32,256]{3,2,1,0:T(8,128)S(1)}, u32[]{:S(2)}, u32[]{:S(2)}) %collective-permute-start.4) | collective-permute-done | bytes 524320 | tf_op jit(solution)/shard_map/ppermute | solution.py:16
  73.0 3.4 %collective-permute-start.6 = (f32[2,8,32,256]{3,2,1,0:T(8,128)S(1)}, f32[2,8,32,256]{3,2,1,0:T(8,128)S(1)}, u32[]{:S(2)}, u32[]{:S(2)}) collective-permute-start(f32[2,8,32,256]{3,2,1,0:T(8,128)S(1)} %collective-permute-done.5.refs_6_), channel_id=1, source_target_pairs={{0,2},{2,0},{32,34},{34,32},{1,3},{3,1},{33,35},{35,33},{4,6},{6,4... | collective-permute-start | bytes 1572872 | tf_op jit(solution)/shard_map/ppermute | solution.py:16
  78.4 7.6 %collective-permute-done.6.refs_4_ = f32[2,8,32,256]{3,2,1,0:T(8,128)S(1)} collective-permute-done((f32[2,8,32,256]{3,2,1,0:T(8,128)S(1)}, f32[2,8,32,256]{3,2,1,0:T(8,128)S(1)}, u32[]{:S(2)}, u32[]{:S(2)}) %collective-permute-start.6) | collective-permute-done | bytes 524320 | tf_op jit(solution)/shard_map/ppermute | solution.py:16
  86.0 3.2 %collective-permute-start.32 = (f32[8,16,512]{2,1,0:T(8,128)S(1)}, f32[8,16,512]{2,1,0:T(8,128)S(1)}, u32[]{:S(2)}, u32[]{:S(2)}) collective-permute-start(f32[8,16,512]{2,1,0:T(8,128)S(1)} %collective-permute-done.23), channel_id=1, source_target_pairs={{0,28},{4,0},{8,4},{12,8},{16,12},{20,16},{24,20},{28,24},{1,29},{... | collective-permute-start | bytes 786440 | tf_op jit(solution)/shard_map/ppermute | solution.py:21
  89.8 3.2 %collective-permute-done.32 = f32[8,16,512]{2,1,0:T(8,128)S(1)} collective-permute-done((f32[8,16,512]{2,1,0:T(8,128)S(1)}, f32[8,16,512]{2,1,0:T(8,128)S(1)}, u32[]{:S(2)}, u32[]{:S(2)}) %collective-permute-start.32) | collective-permute-done | bytes 262176 | tf_op jit(solution)/shard_map/ppermute | solution.py:21
  93.1 4.7 %product.2 = f32[512,512]{1,0:T(8,128)S(1)} custom-call(bf16[512,2048]{1,0:T(8,128)(2,1)S(1)} %get-tuple-element.7.ah, bf16[512,2048]{1,0:T(8,128)(2,1)S(1)} %get-tuple-element.8.al, f32[2,8,16,512]{3,2,1,0:T(8,128)S(1)} %pad_maximum_fusion.6.refs_0_, f32[4,8,16,512]{3,2,1,0:T(8,128)S(1)} %pad_maximum_fusion.refs_1_, ...), custom_call_target="tpu_custom_call" | custom-call | tf_op jit(solution)/shard_map/product/pallas_call | solution.py:98
  99.4 4.7 %product.3 = f32[512,512]{1,0:T(8,128)S(1)} custom-call(bf16[512,2048]{1,0:T(8,128)(2,1)S(1)} %get-tuple-element.7.ah, bf16[512,2048]{1,0:T(8,128)(2,1)S(1)} %get-tuple-element.8.al, f32[2,8,16,512]{3,2,1,0:T(8,128)S(1)} %pad_maximum_fusion.6.refs_0_, f32[4,8,16,512]{3,2,1,0:T(8,128)S(1)} %pad_maximum_fusion.refs_1_, ...), custom_call_target="tpu_custom_call" | custom-call | tf_op jit(solution)/shard_map/product/pallas_call | solution.py:98
  104.2 2.2 %collective-permute-start.34 = (f32[2,4,32,512]{3,2,1,0:T(8,128)S(1)}, f32[2,4,32,512]{3,2,1,0:T(8,128)S(1)}, u32[]{:S(2)}, u32[]{:S(2)}) collective-permute-start(f32[2,4,32,512]{3,2,1,0:T(8,128)S(1)} %pad_maximum_fusion.8), channel_id=1, source_target_pairs={{0,192},{64,128},{128,64},{192,0},{1,193},{65,129},{129,65},{193,1... | collective-permute-start | bytes 1572872 | tf_op jit(solution)/shard_map/ppermute | solution.py:16
  106.4 5.9 %collective-permute-done.30 = f32[2,4,32,512]{3,2,1,0:T(8,128)S(1)} collective-permute-done((f32[2,4,32,512]{3,2,1,0:T(8,128)S(1)}, f32[2,4,32,512]{3,2,1,0:T(8,128)S(1)}, u32[]{:S(2)}, u32[]{:S(2)}) %collective-permute-start.30) | collective-permute-done | bytes 524320 | tf_op jit(solution)/shard_map/ppermute | solution.py:16
  112.3 2.8 %collective-permute-start.31 = (f32[4,32,512]{2,1,0:T(8,128)S(1)}, f32[4,32,512]{2,1,0:T(8,128)S(1)}, u32[]{:S(2)}, u32[]{:S(2)}) collective-permute-start(f32[4,32,512]{2,1,0:T(8,128)S(1)} %fusion.19), channel_id=1, source_target_pairs={{0,192},{64,128},{128,64},{192,0},{1,193},{65,129},{129,65},{193,1... | collective-permute-start | bytes 786440 | tf_op jit(solution)/shard_map/ppermute | solution.py:16
  115.1 5.1 %collective-permute-done.34 = f32[2,4,32,512]{3,2,1,0:T(8,128)S(1)} collective-permute-done((f32[2,4,32,512]{3,2,1,0:T(8,128)S(1)}, f32[2,4,32,512]{3,2,1,0:T(8,128)S(1)}, u32[]{:S(2)}, u32[]{:S(2)}) %collective-permute-start.34) | collective-permute-done | bytes 524320 | tf_op jit(solution)/shard_map/ppermute | solution.py:16
  120.4 4.7 %collective-permute-done.31 = f32[4,32,512]{2,1,0:T(8,128)S(1)} collective-permute-done((f32[4,32,512]{2,1,0:T(8,128)S(1)}, f32[4,32,512]{2,1,0:T(8,128)S(1)}, u32[]{:S(2)}, u32[]{:S(2)}) %collective-permute-start.31) | collective-permute-done | bytes 262176 | tf_op jit(solution)/shard_map/ppermute | solution.py:16
  135.4 2.3 %collective-permute-done.37 = f32[32,1024]{1,0:T(8,128)S(1)} collective-permute-done((f32[32,1024]{1,0:T(8,128)S(1)}, f32[32,1024]{1,0:T(8,128)S(1)}, u32[]{:S(2)}, u32[]{:S(2)}) %collective-permute-start.37) | collective-permute-done | bytes 131104 | tf_op jit(solution)/shard_map/ppermute | solution.py:16
  (99 shorter events, 40.1 us)
Async XLA Ops:
  9.4 15.0 %collective-permute-start = (f32[8,32,256]{2,1,0:T(8,128)S(1)}, f32[8,32,256]{2,1,0:T(8,128)S(1)}, u32[]{:S(2)}, u32[]{:S(2)}) collective-permute-start(f32[8,32,256]{2,1,0:T(8,128)S(1)} %get-tuple-element.16), channel_id=1, source_target_pairs={{0,64},{64,0},{128,192},{192,128},{1,65},{65,1},{129,193},{193,129... | collective-permute-start | bytes 786440 | tf_op jit(solution)/shard_map/ppermute | solution.py:16
  12.9 12.1 %collective-permute-start.15 = (f32[8,16,512]{2,1,0:T(8,128)S(1)}, f32[8,16,512]{2,1,0:T(8,128)S(1)}, u32[]{:S(2)}, u32[]{:S(2)}) collective-permute-start(f32[8,16,512]{2,1,0:T(8,128)S(1)} %get-tuple-element.28), channel_id=1, source_target_pairs={{0,28},{4,0},{8,4},{12,8},{16,12},{20,16},{24,20},{28,24},{1,29},{... | collective-permute-start | bytes 786440 | tf_op jit(solution)/shard_map/ppermute | solution.py:21
  18.4 10.4 %collective-permute-start.14 = (f32[8,16,512]{2,1,0:T(8,128)S(1)}, f32[8,16,512]{2,1,0:T(8,128)S(1)}, u32[]{:S(2)}, u32[]{:S(2)}) collective-permute-start(f32[8,16,512]{2,1,0:T(8,128)S(1)} %get-tuple-element.28), channel_id=1, source_target_pairs={{0,4},{4,8},{8,12},{12,16},{16,20},{20,24},{24,28},{28,0},{1,5},{5... | collective-permute-start | bytes 786440 | tf_op jit(solution)/shard_map/ppermute | solution.py:21
  18.4 12.3 %collective-permute-start.13 = (f32[8,16,512]{2,1,0:T(8,128)S(1)}, f32[8,16,512]{2,1,0:T(8,128)S(1)}, u32[]{:S(2)}, u32[]{:S(2)}) collective-permute-start(f32[8,16,512]{2,1,0:T(8,128)S(1)} %get-tuple-element.25), channel_id=1, source_target_pairs={{0,28},{4,0},{8,4},{12,8},{16,12},{20,16},{24,20},{28,24},{1,29},{... | collective-permute-start | bytes 786440 | tf_op jit(solution)/shard_map/ppermute | solution.py:21
  21.6 12.8 %collective-permute-start.2 = (f32[8,32,256]{2,1,0:T(8,128)S(1)}, f32[8,32,256]{2,1,0:T(8,128)S(1)}, u32[]{:S(2)}, u32[]{:S(2)}) collective-permute-start(f32[8,32,256]{2,1,0:T(8,128)S(1)} %get-tuple-element.18), channel_id=1, source_target_pairs={{0,192},{64,128},{128,64},{192,0},{1,193},{65,129},{129,65},{193,1... | collective-permute-start | bytes 786440 | tf_op jit(solution)/shard_map/ppermute | solution.py:16
  24.4 13.0 %collective-permute-start.12 = (f32[8,16,512]{2,1,0:T(8,128)S(1)}, f32[8,16,512]{2,1,0:T(8,128)S(1)}, u32[]{:S(2)}, u32[]{:S(2)}) collective-permute-start(f32[8,16,512]{2,1,0:T(8,128)S(1)} %get-tuple-element.25), channel_id=1, source_target_pairs={{0,4},{4,8},{8,12},{12,16},{16,20},{20,24},{24,28},{28,0},{1,5},{5... | collective-permute-start | bytes 786440 | tf_op jit(solution)/shard_map/ppermute | solution.py:21
  25.1 12.3 %collective-permute-start.19 = (f32[8,16,512]{2,1,0:T(8,128)S(1)}, f32[8,16,512]{2,1,0:T(8,128)S(1)}, u32[]{:S(2)}, u32[]{:S(2)}) collective-permute-start(f32[8,16,512]{2,1,0:T(8,128)S(1)} %collective-permute-done.15), channel_id=1, source_target_pairs={{0,28},{4,0},{8,4},{12,8},{16,12},{20,16},{24,20},{28,24},{1,29},{... | collective-permute-start | bytes 786440 | tf_op jit(solution)/shard_map/ppermute | solution.py:21
  28.8 11.9 %collective-permute-start.18 = (f32[8,16,512]{2,1,0:T(8,128)S(1)}, f32[8,16,512]{2,1,0:T(8,128)S(1)}, u32[]{:S(2)}, u32[]{:S(2)}) collective-permute-start(f32[8,16,512]{2,1,0:T(8,128)S(1)} %collective-permute-done.14), channel_id=1, source_target_pairs={{0,4},{4,8},{8,12},{12,16},{16,20},{20,24},{24,28},{28,0},{1,5},{5... | collective-permute-start | bytes 786440 | tf_op jit(solution)/shard_map/ppermute | solution.py:21
  30.7 11.2 %collective-permute-start.17 = (f32[8,16,512]{2,1,0:T(8,128)S(1)}, f32[8,16,512]{2,1,0:T(8,128)S(1)}, u32[]{:S(2)}, u32[]{:S(2)}) collective-permute-start(f32[8,16,512]{2,1,0:T(8,128)S(1)} %collective-permute-done.13), channel_id=1, source_target_pairs={{0,28},{4,0},{8,4},{12,8},{16,12},{20,16},{24,20},{28,24},{1,29},{... | collective-permute-start | bytes 786440 | tf_op jit(solution)/shard_map/ppermute | solution.py:21
  34.4 11.3 %collective-permute-start.1 = (f32[8,32,256]{2,1,0:T(8,128)S(1)}, f32[8,32,256]{2,1,0:T(8,128)S(1)}, u32[]{:S(2)}, u32[]{:S(2)}) collective-permute-start(f32[8,32,256]{2,1,0:T(8,128)S(1)} %get-tuple-element.15), channel_id=1, source_target_pairs={{0,128},{64,192},{128,0},{192,64},{1,129},{65,193},{129,1},{193,65... | collective-permute-start | bytes 786440 | tf_op jit(solution)/shard_map/ppermute | solution.py:16
  45.7 11.4 %collective-permute-start.25 = (f32[2,8,16,512]{3,2,1,0:T(8,128)S(1)}, f32[2,8,16,512]{3,2,1,0:T(8,128)S(1)}, u32[]{:S(2)}, u32[]{:S(2)}) collective-permute-start(f32[2,8,16,512]{3,2,1,0:T(8,128)S(1)} %pad_maximum_fusion.6.refs_0_), channel_id=1, source_target_pairs={{0,1},{1,0},{2,3},{3,2},{4,5},{5,4},{6,7},{7,6},{8,9},{9,8},{10,11... | collective-permute-start | bytes 1572872 | tf_op jit(solution)/shard_map/ppermute | solution.py:16
  47.6 14.8 %collective-permute-start.3 = (f32[2,8,32,256]{3,2,1,0:T(8,128)S(1)}, f32[2,8,32,256]{3,2,1,0:T(8,128)S(1)}, u32[]{:S(2)}, u32[]{:S(2)}) collective-permute-start(f32[2,8,32,256]{3,2,1,0:T(8,128)S(1)} %pad_maximum_fusion.3.refs_0_), channel_id=1, source_target_pairs={{0,2},{2,0},{32,34},{34,32},{1,3},{3,1},{33,35},{35,33},{4,6},{6,4... | collective-permute-start | bytes 1572872 | tf_op jit(solution)/shard_map/ppermute | solution.py:16
  49.1 22.4 %collective-permute-start.4 = (f32[2,8,32,256]{3,2,1,0:T(8,128)S(1)}, f32[2,8,32,256]{3,2,1,0:T(8,128)S(1)}, u32[]{:S(2)}, u32[]{:S(2)}) collective-permute-start(f32[2,8,32,256]{3,2,1,0:T(8,128)S(1)} %pad_maximum_fusion.4.refs_1_), channel_id=1, source_target_pairs={{0,2},{2,0},{32,34},{34,32},{1,3},{3,1},{33,35},{35,33},{4,6},{6,4... | collective-permute-start | bytes 1572872 | tf_op jit(solution)/shard_map/ppermute | solution.py:16
  50.3 21.2 %collective-permute-start.5 = (f32[2,8,32,256]{3,2,1,0:T(8,128)S(1)}, f32[2,8,32,256]{3,2,1,0:T(8,128)S(1)}, u32[]{:S(2)}, u32[]{:S(2)}) collective-permute-start(f32[2,8,32,256]{3,2,1,0:T(8,128)S(1)} %pad_maximum_fusion.3.refs_0_), channel_id=1, source_target_pairs={{0,34},{2,32},{32,2},{34,0},{1,35},{3,33},{33,3},{35,1},{4,38},{6,... | collective-permute-start | bytes 1572872 | tf_op jit(solution)/shard_map/ppermute | solution.py:16
  55.8 17.3 %collective-permute-start.8 = (f32[2,8,32,256]{3,2,1,0:T(8,128)S(1)}, f32[2,8,32,256]{3,2,1,0:T(8,128)S(1)}, u32[]{:S(2)}, u32[]{:S(2)}) collective-permute-start(f32[2,8,32,256]{3,2,1,0:T(8,128)S(1)} %pad_maximum_fusion.4.refs_1_), channel_id=1, source_target_pairs={{0,34},{2,32},{32,2},{34,0},{1,35},{3,33},{33,3},{35,1},{4,38},{6,... | collective-permute-start | bytes 1572872 | tf_op jit(solution)/shard_map/ppermute | solution.py:16
  57.2 35.9 %collective-permute-start.26 = (f32[4,8,16,512]{3,2,1,0:T(8,128)S(1)}, f32[4,8,16,512]{3,2,1,0:T(8,128)S(1)}, u32[]{:S(2)}, u32[]{:S(2)}) collective-permute-start(f32[4,8,16,512]{3,2,1,0:T(8,128)S(1)} %pad_maximum_fusion.refs_1_), channel_id=1, source_target_pairs={{0,1},{1,0},{2,3},{3,2},{4,5},{5,4},{6,7},{7,6},{8,9},{9,8},{10,11... | collective-permute-start | bytes 3145736 | tf_op jit(solution)/shard_map/ppermute | solution.py:16
  62.4 14.1 %collective-permute-start.24 = (f32[8,16,512]{2,1,0:T(8,128)S(1)}, f32[8,16,512]{2,1,0:T(8,128)S(1)}, u32[]{:S(2)}, u32[]{:S(2)}) collective-permute-start(f32[8,16,512]{2,1,0:T(8,128)S(1)} %collective-permute-done.20), channel_id=1, source_target_pairs={{0,4},{4,8},{8,12},{12,16},{16,20},{20,24},{24,28},{28,0},{1,5},{5... | collective-permute-start | bytes 786440 | tf_op jit(solution)/shard_map/ppermute | solution.py:21
  71.5 21.5 %collective-permute-start.27 = (f32[4,8,16,512]{3,2,1,0:T(8,128)S(1)}, f32[4,8,16,512]{3,2,1,0:T(8,128)S(1)}, u32[]{:S(2)}, u32[]{:S(2)}) collective-permute-start(f32[4,8,16,512]{3,2,1,0:T(8,128)S(1)} %pad_maximum_fusion.1.refs_2_), channel_id=1, source_target_pairs={{0,1},{1,0},{2,3},{3,2},{4,5},{5,4},{6,7},{7,6},{8,9},{9,8},{10,11... | collective-permute-start | bytes 3145736 | tf_op jit(solution)/shard_map/ppermute | solution.py:16
  71.5 21.5 %collective-permute-start.28 = (f32[4,8,16,512]{3,2,1,0:T(8,128)S(1)}, f32[4,8,16,512]{3,2,1,0:T(8,128)S(1)}, u32[]{:S(2)}, u32[]{:S(2)}) collective-permute-start(f32[4,8,16,512]{3,2,1,0:T(8,128)S(1)} %pad_maximum_fusion.2.refs_3_), channel_id=1, source_target_pairs={{0,1},{1,0},{2,3},{3,2},{4,5},{5,4},{6,7},{7,6},{8,9},{9,8},{10,11... | collective-permute-start | bytes 3145736 | tf_op jit(solution)/shard_map/ppermute | solution.py:16
  73.0 13.0 %collective-permute-start.6 = (f32[2,8,32,256]{3,2,1,0:T(8,128)S(1)}, f32[2,8,32,256]{3,2,1,0:T(8,128)S(1)}, u32[]{:S(2)}, u32[]{:S(2)}) collective-permute-start(f32[2,8,32,256]{3,2,1,0:T(8,128)S(1)} %collective-permute-done.5.refs_6_), channel_id=1, source_target_pairs={{0,2},{2,0},{32,34},{34,32},{1,3},{3,1},{33,35},{35,33},{4,6},{6,4... | collective-permute-start | bytes 1572872 | tf_op jit(solution)/shard_map/ppermute | solution.py:16
  76.5 12.7 %collective-permute-start.7 = (f32[2,8,32,256]{3,2,1,0:T(8,128)S(1)}, f32[2,8,32,256]{3,2,1,0:T(8,128)S(1)}, u32[]{:S(2)}, u32[]{:S(2)}) collective-permute-start(f32[2,8,32,256]{3,2,1,0:T(8,128)S(1)} %collective-permute-done.4.refs_3_), channel_id=1, source_target_pairs={{0,34},{2,32},{32,2},{34,0},{1,35},{3,33},{33,3},{35,1},{4,38},{6,... | collective-permute-start | bytes 1572872 | tf_op jit(solution)/shard_map/ppermute | solution.py:16
  97.9 14.4 %collective-permute-start.30 = (f32[2,4,32,512]{3,2,1,0:T(8,128)S(1)}, f32[2,4,32,512]{3,2,1,0:T(8,128)S(1)}, u32[]{:S(2)}, u32[]{:S(2)}) collective-permute-start(f32[2,4,32,512]{3,2,1,0:T(8,128)S(1)} %pad_maximum_fusion.7), channel_id=1, source_target_pairs={{0,64},{64,0},{128,192},{192,128},{1,65},{65,1},{129,193},{193,129... | collective-permute-start | bytes 1572872 | tf_op jit(solution)/shard_map/ppermute | solution.py:16
  104.2 16.1 %collective-permute-start.34 = (f32[2,4,32,512]{3,2,1,0:T(8,128)S(1)}, f32[2,4,32,512]{3,2,1,0:T(8,128)S(1)}, u32[]{:S(2)}, u32[]{:S(2)}) collective-permute-start(f32[2,4,32,512]{3,2,1,0:T(8,128)S(1)} %pad_maximum_fusion.8), channel_id=1, source_target_pairs={{0,192},{64,128},{128,64},{192,0},{1,193},{65,129},{129,65},{193,1... | collective-permute-start | bytes 1572872 | tf_op jit(solution)/shard_map/ppermute | solution.py:16
  112.3 12.9 %collective-permute-start.31 = (f32[4,32,512]{2,1,0:T(8,128)S(1)}, f32[4,32,512]{2,1,0:T(8,128)S(1)}, u32[]{:S(2)}, u32[]{:S(2)}) collective-permute-start(f32[4,32,512]{2,1,0:T(8,128)S(1)} %fusion.19), channel_id=1, source_target_pairs={{0,192},{64,128},{128,64},{192,0},{1,193},{65,129},{129,65},{193,1... | collective-permute-start | bytes 786440 | tf_op jit(solution)/shard_map/ppermute | solution.py:16
  (16 other events, 118.8 us)
where the time goes:
time: 139 us
  waiting for transfers between devices  60.8 us (44%)
  starting transfers between devices  60.4 us (43%)
  Pallas kernels  10 us (7%)
  local copies, waits for them, and re-layouts  4.89 us (4%)
  matrix products  1.69 us (1%)
    ppermute x25, waiting for transfers between devices, swap(): return lax.ppermute(v, axis, [(i, i ^ bits) for i in range(n)])  48.3 us
    ppermute x25, starting transfers between devices, swap(): return lax.ppermute(v, axis, [(i, i ^ bits) for i in range(n)])  34.1 us
    ppermute x14, starting transfers between devices, shift(): return lax.ppermute(v, axis, [(i, (i + step) % n) for i in range(n)])  26.2 us
    ppermute x14, waiting for transfers between devices, shift(): return lax.ppermute(v, axis, [(i, (i + step) % n) for i in range(n)])  12.5 us
    pallas_call x2, Pallas kernels, product(): pl.pallas_call(kernel, out_shape=jax.ShapeDtypeStruct((512, 512), F32), i...  9.36 us
  transfers between devices with their start and end apart: 39, of which 19 were waited for; matrix products, arithmetic and copies ran while one was open for 3% of the time, Pallas kernels for 7%

commit v1 on v0

v1 whole, which is shorter than its diff:
```python
import jax
import jax.numpy as jnp
from jax import lax
from jax.experimental import pallas as pl
from jax.experimental.pallas import tpu as pltpu
from jax.sharding import Mesh
from jax.sharding import PartitionSpec as P

AXES = ("x", "yh", "z", "yl", "c")
Y = ("yh", "yl")
F32, BF16 = jnp.float32, jnp.bfloat16


EARLY, LATE = (0, 7, 1, 6), (2, 5, 3, 4)

WAYS = ((1, 3), (3, 1))


def swap(v, axis, bits):
    n = lax.axis_size(axis)
    return lax.ppermute(v, axis, [(i, i ^ bits) for i in range(n)])


def shift(v, axis, step):
    n = lax.axis_size(axis)
    return lax.ppermute(v, axis, [(i, (i + step) % n) for i in range(n)])


def pick(pieces, index):
    low = jnp.where(index % 2 == 1, pieces[1], pieces[0])
    high = jnp.where(index % 2 == 1, pieces[3], pieces[2])
    return jnp.where(index >= 2, high, low)


def lane_order(z, c):
    src = lax.broadcasted_iota(jnp.int32, (256, 256), 0)
    dst = lax.broadcasted_iota(jnp.int32, (256, 256), 1)
    yh, zz, yl, cc, q = src // 128, (src // 16) % 8, (src // 8) % 2, (src // 4) % 2, src % 4
    apart = (zz - z) % 8
    place = sum(jnp.where(apart == s, k, 0) for k, s in enumerate(EARLY + LATE))
    to = (place // 4) * 128 + (cc ^ c) * 64 + (place % 4) * 16 + yh * 8 + yl * 4 + q
    return (to == dst).astype(F32)


def parts(v):
    high = v.astype(BF16)
    return high, (v - high.astype(F32)).astype(BF16)


VMEM = pl.BlockSpec(memory_space=pltpu.VMEM)
PARAMS = pltpu.CompilerParams(vmem_limit_bytes=16 * 1024 * 1024)


def column_group():
    return 2 * lax.axis_index("yh") + lax.axis_index("yl")


def cut_right(b):
    def kernel(b_ref, *outs):
        y = column_group()
        for d, out in enumerate(outs):
            k = jnp.bitwise_xor(y, d)
            for i in range(2):
                low, high = b_ref[:, :, k // 2, i, :], b_ref[:, :, k // 2, 2 + i, :]
                out[:, :, pl.ds(512 * i, 512)] = jnp.where(k % 2 == 1, high, low)

    return pl.pallas_call(
        kernel,
        out_shape=(jax.ShapeDtypeStruct((8, 4, 1024), F32),) * 4,
        in_specs=[VMEM],
        out_specs=(VMEM,) * 4,
        compiler_params=PARAMS,
        name="cut_right",
    )(b)


def join_right(got):
    def kernel(*refs):
        y = column_group()
        for k in range(4):
            d = jnp.bitwise_xor(y, k)
            for h in range(2):
                at = pl.ds(512 * h, 512)
                low = jnp.where(d % 2 == 1, refs[1][:, :, at], refs[0][:, :, at])
                high = jnp.where(d % 2 == 1, refs[3][:, :, at], refs[2][:, :, at])
                refs[4 + h][:, pl.ds(4 * k, 4), :] = jnp.where(d >= 2, high, low)

    return pl.pallas_call(
        kernel,
        out_shape=(jax.ShapeDtypeStruct((8, 16, 512), F32),) * 2,
        in_specs=[VMEM] * 4,
        out_specs=(VMEM,) * 2,
        compiler_params=PARAMS,
        name="join_right",
    )(*got)


def split_left(left):
    n = len(left)
    which = [(g, d) for g in range(n) for d in range(left[g].shape[0])]

    def kernel(*refs):
        outs = refs[n:]

        def step(b, carry):
            for k, (g, d) in enumerate(which):
                rows = pl.ds(32 * k, 32)
                for phase in range(2):
                    high, low = parts(refs[g][d, b, :, pl.ds(128 * phase, 128)])
                    for k3, v in enumerate((high, high, low)):
                        at = pl.ds(pl.multiple_of(1024 * k3 + b * 128, 128), 128)
                        outs[phase][rows, at] = v
            return carry

        lax.fori_loop(0, 8, step, 0)

    return pl.pallas_call(
        kernel,
        out_shape=(jax.ShapeDtypeStruct((32 * len(which), 3072), BF16),) * 2,
        in_specs=[VMEM] * n,
        out_specs=(VMEM,) * 2,
        compiler_params=PARAMS,
        name="split_left",
    )(*left)


def sources(blocks):
    arrays = []
    for v, _ in blocks:
        if not any(v is w for w in arrays):
            arrays.append(v)
    return arrays, [(next(k for k, w in enumerate(arrays) if w is v), i) for v, i in blocks]


def stack_right(to, where, refs, b, column=0):
    for k, (r, i) in enumerate(where):
        high, low = parts(refs[r][i, b])
        for k3, v in enumerate((high, low, high)):
            at = pl.ds(pl.multiple_of(1024 * k3 + b * 128 + k * 16, 16), 16)
            to[at, pl.ds(column, 512)] = v


def product(left, right):
    return jnp.dot(left, right, preferred_element_type=F32)


def early_product(left, blocks):
    arrays, where = sources(blocks[0] + blocks[1])
    n = len(arrays)

    def kernel(a, *refs):
        o_ref, right = refs[n:]

        def split(b, carry):
            for h in range(2):
                stack_right(right, where[8 * h : 8 * h + 8], refs, b, 512 * h)
            return carry

        lax.fori_loop(0, 8, split, 0)

        def columns(h, carry):
            at = pl.ds(pl.multiple_of(512 * h, 512), 512)
            o_ref[:, at] = product(a[...], right[:, at])
            return carry

        lax.fori_loop(0, 2, columns, 0)

    return pl.pallas_call(
        kernel,
        out_shape=(
            jax.ShapeDtypeStruct((384, 1024), F32),
            jax.ShapeDtypeStruct((3072, 1024), BF16),
        ),
        in_specs=[VMEM] * (n + 1),
        out_specs=(VMEM,) * 2,
        compiler_params=PARAMS,
        name="early_product",
    )(left, *arrays)


def late_product(near, far, early, blocks, half):
    arrays, where = sources(blocks)
    n = len(arrays)

    def kernel(a, far_early, far_late, total_ref, right_early, *refs):
        outs, right = refs[n : n + 6], refs[n + 6]

        def split(b, carry):
            stack_right(right, where, refs, b)
            return carry

        lax.fori_loop(0, 8, split, 0)
        columns = pl.ds(512 * half, 512)

        def put(slot, total):
            for quarter, (first, second) in enumerate(WAYS):
                keep_ref, pass_ref, send_ref = outs[3 * quarter : 3 * quarter + 3]
                part = total[:, 256 * quarter : 256 * quarter + 256]
                keep_ref[slot] = part[0:32]
                pass_ref[slot] = part[32 * second : 32 * second + 32]
                send_ref[0, slot] = part[32 * first : 32 * first + 32]
                send_ref[1, slot] = part[64:96]

        near_total = product(a[...], right[...]) + total_ref[:, columns]
        for m, slot in enumerate((0, 1, 3)):
            put(slot, near_total[128 * m : 128 * m + 128])
        put(2, product(far_early[...], right_early[:, columns]) + product(far_late[...], right[...]))

    one, two = jax.ShapeDtypeStruct((4, 32, 256), F32), jax.ShapeDtypeStruct((2, 4, 32, 256), F32)
    return pl.pallas_call(
        kernel,
        out_shape=(one, one, two) * 2,
        in_specs=[VMEM] * (n + 5),
        out_specs=(VMEM,) * 6,
        scratch_shapes=[pltpu.VMEM((3072, 512), BF16)],
        compiler_params=PARAMS,
        name="late_product",
    )(near[1], *far, *early, *arrays)


def placed_product(a, b):
    x, z, c = lax.axis_index("x"), lax.axis_index("z"), lax.axis_index("c")
    y = lax.axis_index(Y)

    b_for = cut_right(b)
    b_got = [b_for[0]] + [swap(b_for[d], Y, d) for d in (1, 2, 3)]
    halves = join_right(b_got)

    ordered = jnp.dot(a.reshape(32, 8, 4, 256), lane_order(z, c), precision=lax.Precision.HIGH)
    ordered = jnp.transpose(ordered, (2, 1, 0, 3))
    a_for = [lax.dynamic_index_in_dim(ordered, x ^ d, axis=0, keepdims=False) for d in range(4)]
    a_got = [a_for[0]] + [swap(a_for[d], "x", d) for d in (1, 2, 3)]
    one, rest = a_got[0], jnp.stack(a_got[1:])
    near1 = swap(one, Y, 1), swap(rest, Y, 1)
    near3 = swap(one, Y, 3), swap(rest, Y, 3)
    far_low = swap(jnp.stack([near3[0], near3[1][0]]), Y, 1)
    far_high = swap(near1[1][1:], Y, 3)
    near = split_left([one[None], rest, near1[0][None], near1[1], near3[0][None], near3[1]])
    far = split_left([far_low, far_high])

    own, other = [{}, {}], [{}, {}]
    up, down, held = list(halves), list(halves), list(halves)
    places = [(0, 0), (1, 0)]
    for s in (1, 2, 3):
        for h in range(2):
            up[h] = shift(up[h], "z", 1)
            down[h] = shift(down[h], "z", -1)
        held += [up[0], down[0], up[1], down[1]]
        places += [(0, 8 - s), (0, s), (1, 8 - s), (1, s)]
        if s == 3:
            break
        both = jnp.stack(held)
        crossed = swap(both, "c", 1)
        for i, (h, at) in enumerate(places):
            own[h][at], other[h][at] = (both, i), (crossed, i)
        held, places = [], []
    early = early_product(
        near[0], [[v[h][s] for v in (own, other) for s in EARLY] for h in range(2)]
    )
    held += [shift(up[0], "z", 1), shift(down[1], "z", -1)]
    places += [(0, 4), (1, 4)]
    both = jnp.stack(held)
    crossed = swap(both, "c", 1)
    for i, (h, at) in enumerate(places):
        own[h][at], other[h][at] = (both, i), (crossed, i)

    sums = []
    for h in range(2):
        blocks = [v[h][s] for v in (own, other) for s in LATE]
        pieces = late_product(near, far, early, blocks, h)
        for quarter, (first, second) in enumerate(WAYS):
            keep, pass_on, send = pieces[3 * quarter : 3 * quarter + 3]
            got = swap(send, "x", first)
            sums.append(keep + got[0] + swap(pass_on + got[1], "x", second))
    summed = jnp.concatenate(sums, axis=2)
    back = [summed[0]] + [swap(summed[d], Y, d) for d in (1, 2, 3)]
    placed = jnp.stack([pick(back, y ^ k) for k in range(4)], axis=1)
    return placed.reshape(8, 4, 2, 4, 512)


def solution(mesh):
    split = Mesh(mesh.devices.reshape(4, 2, 8, 2, 2), AXES)
    spec = P(None, AXES, None, None, None)
    return jax.shard_map(placed_product, mesh=split, in_specs=(spec, spec), out_specs=spec, check_vma=False)
```

time: 139 us -> 151 us (1.086)
  waiting for transfers between devices: 60.8 us -> 72.8 us
    ppermute x14, waiting for transfers between devices: 12.5 us -> 19.9 us  [shift(): return lax.ppermute(v, axis, [(i, (i + step) % n) for i in range(n)])]
    ppermute x25 -> x26, waiting for transfers between devices: 48.3 us -> 52.9 us  [swap(): return lax.ppermute(v, axis, [(i, i ^ bits) for i in range(n)])]
    reshape x2 -> x0, local copies, waits for them, and re-layouts: 1.72 us -> none  [the longest x1 1.53 us: placed_product(): bg = b.reshape(8, 4, 4, 1024)]
    ppermute x25 -> x26, starting transfers between devices: 34.1 us -> 33.3 us  [swap(): return lax.ppermute(v, axis, [(i, i ^ bits) for i in range(n)])]
    pallas_call x3 -> x7, Pallas kernels: 10 us -> 10.7 us  [the longest x2 5.13 us: late_product(): pl.pallas_call(kernel, out_shape=(one, one, two) * 2, in_specs=[VMEM] * (...]
  transfers between devices with their start and end apart: 39 -> 40, of which waited for: 19 -> 24; matrix products, arithmetic and copies ran while one was open for 3% -> 3% of each run, Pallas kernels for 7% -> 5%
where the time goes in v1:
time: 151 us
  waiting for transfers between devices  72.8 us (48%)
  starting transfers between devices  59.7 us (40%)
  Pallas kernels  10.7 us (7%)
  local copies, waits for them, and re-layouts  4.95 us (3%)
    ppermute x26, waiting for transfers between devices, swap(): return lax.ppermute(v, axis, [(i, i ^ bits) for i in range(n)])  52.9 us
    ppermute x26, starting transfers between devices, swap(): return lax.ppermute(v, axis, [(i, i ^ bits) for i in range(n)])  33.3 us
    ppermute x14, starting transfers between devices, shift(): return lax.ppermute(v, axis, [(i, (i + step) % n) for i in range(n)])  26.4 us
    ppermute x14, waiting for transfers between devices, shift(): return lax.ppermute(v, axis, [(i, (i + step) % n) for i in range(n)])  19.9 us
    pallas_call x2, Pallas kernels, late_product(): pl.pallas_call(kernel, out_shape=(one, one, two) * 2, in_specs=[VMEM] * (...  5.13 us
    pallas_call x1, Pallas kernels, early_product(): pl.pallas_call(kernel, out_shape=(jax.ShapeDtypeStruct((384, 1024), F32),...  3.43 us
  transfers between devices with their start and end apart: 40, of which 24 were waited for; matrix products, arithmetic and copies ran while one was open for 3% of the time, Pallas kernels for 5%

profile of v1, /device:TPU:8, one launch (start us, length us, event | category | flops | bytes accessed | tf_op | source)
XLA Modules:
  0.0 150.6 jit_solution(4293271126505929821)
XLA Ops:
  8.6 2.6 %collective-permute-start.2 = (f32[8,32,256]{2,1,0:T(8,128)S(1)}, f32[8,32,256]{2,1,0:T(8,128)S(1)}, u32[]{:S(2)}, u32[]{:S(2)}) collective-permute-start(f32[8,32,256]{2,1,0:T(8,128)S(1)} %get-tuple-element.57), channel_id=1, source_target_pairs={{0,192},{64,128},{128,64},{192,0},{1,193},{65,129},{129,65},{193,1... | collective-permute-start | bytes 786440 | tf_op jit(solution)/shard_map/ppermute | solution.py:21
  14.8 4.0 %collective-permute-start.13 = (f32[8,16,512]{2,1,0:T(8,128)S(1)}, f32[8,16,512]{2,1,0:T(8,128)S(1)}, u32[]{:S(2)}, u32[]{:S(2)}) collective-permute-start(f32[8,16,512]{2,1,0:T(8,128)S(1)} %get-tuple-element.37), channel_id=1, source_target_pairs={{0,28},{4,0},{8,4},{12,8},{16,12},{20,16},{24,20},{28,24},{1,29},{... | collective-permute-start | bytes 786440 | tf_op jit(solution)/shard_map/ppermute | solution.py:26
  18.8 3.7 %collective-permute-done.2 = f32[8,32,256]{2,1,0:T(8,128)S(1)} collective-permute-done((f32[8,32,256]{2,1,0:T(8,128)S(1)}, f32[8,32,256]{2,1,0:T(8,128)S(1)}, u32[]{:S(2)}, u32[]{:S(2)}) %collective-permute-start.2) | collective-permute-done | bytes 262176 | tf_op jit(solution)/shard_map/ppermute | solution.py:21
  24.4 3.9 %collective-permute-start.15 = (f32[8,16,512]{2,1,0:T(8,128)S(1)}, f32[8,16,512]{2,1,0:T(8,128)S(1)}, u32[]{:S(2)}, u32[]{:S(2)}) collective-permute-start(f32[8,16,512]{2,1,0:T(8,128)S(1)} %get-tuple-element.38), channel_id=1, source_target_pairs={{0,28},{4,0},{8,4},{12,8},{16,12},{20,16},{24,20},{28,24},{1,29},{... | collective-permute-start | bytes 786440 | tf_op jit(solution)/shard_map/ppermute | solution.py:26
  30.2 2.5 %collective-permute-done.15 = f32[8,16,512]{2,1,0:T(8,128)S(1)} collective-permute-done((f32[8,16,512]{2,1,0:T(8,128)S(1)}, f32[8,16,512]{2,1,0:T(8,128)S(1)}, u32[]{:S(2)}, u32[]{:S(2)}) %collective-permute-start.15) | collective-permute-done | bytes 262176 | tf_op jit(solution)/shard_map/ppermute | solution.py:26
  32.7 3.7 %collective-permute-start.19 = (f32[8,16,512]{2,1,0:T(8,128)S(1)}, f32[8,16,512]{2,1,0:T(8,128)S(1)}, u32[]{:S(2)}, u32[]{:S(2)}) collective-permute-start(f32[8,16,512]{2,1,0:T(8,128)S(1)} %collective-permute-done.15), channel_id=1, source_target_pairs={{0,28},{4,0},{8,4},{12,8},{16,12},{20,16},{24,20},{28,24},{1,29},{... | collective-permute-start | bytes 786440 | tf_op jit(solution)/shard_map/ppermute | solution.py:26
  40.2 5.3 %collective-permute-done.17 = f32[8,16,512]{2,1,0:T(8,128)S(1)} collective-permute-done((f32[8,16,512]{2,1,0:T(8,128)S(1)}, f32[8,16,512]{2,1,0:T(8,128)S(1)}, u32[]{:S(2)}, u32[]{:S(2)}) %collective-permute-start.17) | collective-permute-done | bytes 262176 | tf_op jit(solution)/shard_map/ppermute | solution.py:26
  45.5 3.7 %collective-permute-start.23 = (f32[8,16,512]{2,1,0:T(8,128)S(1)}, f32[8,16,512]{2,1,0:T(8,128)S(1)}, u32[]{:S(2)}, u32[]{:S(2)}) collective-permute-start(f32[8,16,512]{2,1,0:T(8,128)S(1)} %collective-permute-done.17), channel_id=1, source_target_pairs={{0,28},{4,0},{8,4},{12,8},{16,12},{20,16},{24,20},{28,24},{1,29},{... | collective-permute-start | bytes 786440 | tf_op jit(solution)/shard_map/ppermute | solution.py:26
  51.4 3.1 %collective-permute-done.23 = f32[8,16,512]{2,1,0:T(8,128)S(1)} collective-permute-done((f32[8,16,512]{2,1,0:T(8,128)S(1)}, f32[8,16,512]{2,1,0:T(8,128)S(1)}, u32[]{:S(2)}, u32[]{:S(2)}) %collective-permute-start.23) | collective-permute-done | bytes 262176 | tf_op jit(solution)/shard_map/ppermute | solution.py:26
  54.8 2.7 %collective-permute-done.25 = f32[8,16,512]{2,1,0:T(8,128)S(1)} collective-permute-done((f32[8,16,512]{2,1,0:T(8,128)S(1)}, f32[8,16,512]{2,1,0:T(8,128)S(1)}, u32[]{:S(2)}, u32[]{:S(2)}) %collective-permute-start.25) | collective-permute-done | bytes 262176 | tf_op jit(solution)/shard_map/ppermute | solution.py:26
  57.6 3.7 %collective-permute-start.27 = (f32[8,16,512]{2,1,0:T(8,128)S(1)}, f32[8,16,512]{2,1,0:T(8,128)S(1)}, u32[]{:S(2)}, u32[]{:S(2)}) collective-permute-start(f32[8,16,512]{2,1,0:T(8,128)S(1)} %collective-permute-done.25), channel_id=1, source_target_pairs={{0,28},{4,0},{8,4},{12,8},{16,12},{20,16},{24,20},{28,24},{1,29},{... | collective-permute-start | bytes 786440 | tf_op jit(solution)/shard_map/ppermute | solution.py:26
  61.4 3.5 %collective-permute-done.26 = f32[8,16,512]{2,1,0:T(8,128)S(1)} collective-permute-done((f32[8,16,512]{2,1,0:T(8,128)S(1)}, f32[8,16,512]{2,1,0:T(8,128)S(1)}, u32[]{:S(2)}, u32[]{:S(2)}) %collective-permute-start.26) | collective-permute-done | bytes 262176 | tf_op jit(solution)/shard_map/ppermute | solution.py:26
  69.5 6.5 %collective-permute-done.5 = f32[8,32,256]{2,1,0:T(8,128)S(1)} collective-permute-done((f32[8,32,256]{2,1,0:T(8,128)S(1)}, f32[8,32,256]{2,1,0:T(8,128)S(1)}, u32[]{:S(2)}, u32[]{:S(2)}) %collective-permute-start.5) | collective-permute-done | bytes 262176 | tf_op jit(solution)/shard_map/ppermute | solution.py:21
  77.0 8.8 %collective-permute-done.4.refs_3_ = f32[3,8,32,256]{3,2,1,0:T(8,128)S(1)} collective-permute-done((f32[3,8,32,256]{3,2,1,0:T(8,128)S(1)}, f32[3,8,32,256]{3,2,1,0:T(8,128)S(1)}, u32[]{:S(2)}, u32[]{:S(2)}) %collective-permute-start.4) | collective-permute-done | bytes 786464 | tf_op jit(solution)/shard_map/ppermute | solution.py:21
  87.6 3.8 %collective-permute-done.3 = f32[8,32,256]{2,1,0:T(8,128)S(1)} collective-permute-done((f32[8,32,256]{2,1,0:T(8,128)S(1)}, f32[8,32,256]{2,1,0:T(8,128)S(1)}, u32[]{:S(2)}, u32[]{:S(2)}) %collective-permute-start.3) | collective-permute-done | bytes 262176 | tf_op jit(solution)/shard_map/ppermute | solution.py:21
  94.9 7.2 %collective-permute-done.7.refs_0_ = f32[2,8,32,256]{3,2,1,0:T(8,128)S(1)} collective-permute-done((f32[2,8,32,256]{3,2,1,0:T(8,128)S(1)}, f32[2,8,32,256]{3,2,1,0:T(8,128)S(1)}, u32[]{:S(2)}, u32[]{:S(2)}) %collective-permute-start.7) | collective-permute-done | bytes 524320 | tf_op jit(solution)/shard_map/ppermute | solution.py:21
  102.1 3.0 %collective-permute-done.8.refs_1_ = f32[2,8,32,256]{3,2,1,0:T(8,128)S(1)} collective-permute-done((f32[2,8,32,256]{3,2,1,0:T(8,128)S(1)}, f32[2,8,32,256]{3,2,1,0:T(8,128)S(1)}, u32[]{:S(2)}, u32[]{:S(2)}) %collective-permute-start.8) | collective-permute-done | bytes 524320 | tf_op jit(solution)/shard_map/ppermute | solution.py:21
  105.5 3.4 %early_product.1 = (f32[384,1024]{1,0:T(8,128)S(1)}, bf16[3072,1024]{1,0:T(8,128)(2,1)S(1)}) custom-call(bf16[384,3072]{1,0:T(8,128)(2,1)S(1)} %get-tuple-element.32.a, f32[6,8,16,512]{3,2,1,0:T(8,128)S(1)} %bitcast_dynamic-update-slice_fusion.6.refs_0_, f32[4,8,16,512]{3,2,1,0:T(8,128)S(1)} %pad_maximum_fusion.refs_1_.refs_0_, ...), custom_call_target="tpu_custom_call" | custom-call | tf_op jit(solution)/shard_map/early_product/pallas_call | solution.py:168
  109.0 2.6 %late_product.3 = (f32[4,32,256]{2,1,0:T(8,128)S(1)}, f32[4,32,256]{2,1,0:T(8,128)S(1)}, f32[2,4,32,256]{3,2,1,0:T(8,128)S(1)}, f32[4,32,256]{2,1,0:T(8,128)S(1)...) custom-call(bf16[384,3072]{1,0:T(8,128)(2,1)S(1)} %get-tuple-element.29.a, ...), custom_call_target="tpu_custom_call" | custom-call | tf_op jit(solution)/shard_map/late_product/pallas_call | solution.py:210
  111.6 5.5 %collective-permute-start.35 = (f32[2,4,32,256]{3,2,1,0:T(8,128)S(1)}, f32[2,4,32,256]{3,2,1,0:T(8,128)S(1)}, u32[]{:S(2)}, u32[]{:S(2)}) collective-permute-start(f32[2,4,32,256]{3,2,1,0:T(8,128)S(1)} %get-tuple-element.51), channel_id=1, source_target_pairs={{0,192},{64,128},{128,64},{192,0},{1,193},{65,129},{129,65},{193,1... | collective-permute-start | bytes 786440 | tf_op jit(solution)/shard_map/ppermute | solution.py:21
  117.0 2.6 %late_product.2 = (f32[4,32,256]{2,1,0:T(8,128)S(1)}, f32[4,32,256]{2,1,0:T(8,128)S(1)}, f32[2,4,32,256]{3,2,1,0:T(8,128)S(1)}, f32[4,32,256]{2,1,0:T(8,128)S(1)...) custom-call(bf16[384,3072]{1,0:T(8,128)(2,1)S(1)} %get-tuple-element.29.a, ...), custom_call_target="tpu_custom_call" | custom-call | tf_op jit(solution)/shard_map/late_product/pallas_call | solution.py:210
  123.9 2.4 %collective-permute-done.33 = f32[2,4,32,256]{3,2,1,0:T(8,128)S(1)} collective-permute-done((f32[2,4,32,256]{3,2,1,0:T(8,128)S(1)}, f32[2,4,32,256]{3,2,1,0:T(8,128)S(1)}, u32[]{:S(2)}, u32[]{:S(2)}) %collective-permute-start.33) | collective-permute-done | bytes 262176 | tf_op jit(solution)/shard_map/ppermute | solution.py:21
  135.2 2.9 %collective-permute-done.30 = f32[4,32,256]{2,1,0:T(8,128)S(1)} collective-permute-done((f32[4,32,256]{2,1,0:T(8,128)S(1)}, f32[4,32,256]{2,1,0:T(8,128)S(1)}, u32[]{:S(2)}, u32[]{:S(2)}) %collective-permute-start.30) | collective-permute-done | bytes 131104 | tf_op jit(solution)/shard_map/ppermute | solution.py:21
  145.4 3.5 %collective-permute-done.38 = f32[32,1024]{1,0:T(8,128)S(1)} collective-permute-done((f32[32,1024]{1,0:T(8,128)S(1)}, f32[32,1024]{1,0:T(8,128)S(1)}, u32[]{:S(2)}, u32[]{:S(2)}) %collective-permute-start.38) | collective-permute-done | bytes 131104 | tf_op jit(solution)/shard_map/ppermute | solution.py:21
  (107 shorter events, 55.4 us)
Async XLA Ops:
  1.2 10.8 %collective-permute-start.9 = (f32[8,4,1024]{2,1,0:T(4,128)S(1)}, f32[8,4,1024]{2,1,0:T(4,128)S(1)}, u32[]{:S(2)}, u32[]{:S(2)}) collective-permute-start(f32[8,4,1024]{2,1,0:T(4,128)S(1)} %get-tuple-element.34), channel_id=1, source_target_pairs={{0,2},{2,0},{32,34},{34,32},{1,3},{3,1},{33,35},{35,33},{4,6},{6,4... | collective-permute-start | bytes 393224 | tf_op jit(solution)/shard_map/ppermute | solution.py:21
  8.6 13.9 %collective-permute-start.2 = (f32[8,32,256]{2,1,0:T(8,128)S(1)}, f32[8,32,256]{2,1,0:T(8,128)S(1)}, u32[]{:S(2)}, u32[]{:S(2)}) collective-permute-start(f32[8,32,256]{2,1,0:T(8,128)S(1)} %get-tuple-element.57), channel_id=1, source_target_pairs={{0,192},{64,128},{128,64},{192,0},{1,193},{65,129},{129,65},{193,1... | collective-permute-start | bytes 786440 | tf_op jit(solution)/shard_map/ppermute | solution.py:21
  11.2 13.2 %collective-permute-start.1 = (f32[8,32,256]{2,1,0:T(8,128)S(1)}, f32[8,32,256]{2,1,0:T(8,128)S(1)}, u32[]{:S(2)}, u32[]{:S(2)}) collective-permute-start(f32[8,32,256]{2,1,0:T(8,128)S(1)} %get-tuple-element.54), channel_id=1, source_target_pairs={{0,128},{64,192},{128,0},{192,64},{1,129},{65,193},{129,1},{193,65... | collective-permute-start | bytes 786440 | tf_op jit(solution)/shard_map/ppermute | solution.py:21
  12.1 16.3 %collective-permute-start = (f32[8,32,256]{2,1,0:T(8,128)S(1)}, f32[8,32,256]{2,1,0:T(8,128)S(1)}, u32[]{:S(2)}, u32[]{:S(2)}) collective-permute-start(f32[8,32,256]{2,1,0:T(8,128)S(1)} %get-tuple-element.55), channel_id=1, source_target_pairs={{0,64},{64,0},{128,192},{192,128},{1,65},{65,1},{129,193},{193,129... | collective-permute-start | bytes 786440 | tf_op jit(solution)/shard_map/ppermute | solution.py:21
  13.0 17.1 %collective-permute-start.12 = (f32[8,16,512]{2,1,0:T(8,128)S(1)}, f32[8,16,512]{2,1,0:T(8,128)S(1)}, u32[]{:S(2)}, u32[]{:S(2)}) collective-permute-start(f32[8,16,512]{2,1,0:T(8,128)S(1)} %get-tuple-element.37), channel_id=1, source_target_pairs={{0,4},{4,8},{8,12},{12,16},{16,20},{20,24},{24,28},{28,0},{1,5},{5... | collective-permute-start | bytes 786440 | tf_op jit(solution)/shard_map/ppermute | solution.py:26
  14.8 21.6 %collective-permute-start.13 = (f32[8,16,512]{2,1,0:T(8,128)S(1)}, f32[8,16,512]{2,1,0:T(8,128)S(1)}, u32[]{:S(2)}, u32[]{:S(2)}) collective-permute-start(f32[8,16,512]{2,1,0:T(8,128)S(1)} %get-tuple-element.37), channel_id=1, source_target_pairs={{0,28},{4,0},{8,4},{12,8},{16,12},{20,16},{24,20},{28,24},{1,29},{... | collective-permute-start | bytes 786440 | tf_op jit(solution)/shard_map/ppermute | solution.py:26
  22.5 14.4 %collective-permute-start.14 = (f32[8,16,512]{2,1,0:T(8,128)S(1)}, f32[8,16,512]{2,1,0:T(8,128)S(1)}, u32[]{:S(2)}, u32[]{:S(2)}) collective-permute-start(f32[8,16,512]{2,1,0:T(8,128)S(1)} %get-tuple-element.38), channel_id=1, source_target_pairs={{0,4},{4,8},{8,12},{12,16},{16,20},{20,24},{24,28},{28,0},{1,5},{5... | collective-permute-start | bytes 786440 | tf_op jit(solution)/shard_map/ppermute | solution.py:26
  28.5 47.6 %collective-permute-start.6 = (f32[3,8,32,256]{3,2,1,0:T(8,128)S(1)}, f32[3,8,32,256]{3,2,1,0:T(8,128)S(1)}, u32[]{:S(2)}, u32[]{:S(2)}) collective-permute-start(f32[3,8,32,256]{3,2,1,0:T(8,128)S(1)} %pad_maximum_fusion.1.refs_1_), channel_id=1, source_target_pairs={{0,34},{2,32},{32,2},{34,0},{1,35},{3,33},{33,3},{35,1},{4,38},{6,... | collective-permute-start | bytes 2359304 | tf_op jit(solution)/shard_map/ppermute | solution.py:21
  30.1 10.0 %collective-permute-start.16 = (f32[8,16,512]{2,1,0:T(8,128)S(1)}, f32[8,16,512]{2,1,0:T(8,128)S(1)}, u32[]{:S(2)}, u32[]{:S(2)}) collective-permute-start(f32[8,16,512]{2,1,0:T(8,128)S(1)} %collective-permute-done.12), channel_id=1, source_target_pairs={{0,4},{4,8},{8,12},{12,16},{16,20},{20,24},{24,28},{28,0},{1,5},{5... | collective-permute-start | bytes 786440 | tf_op jit(solution)/shard_map/ppermute | solution.py:26
  32.7 16.5 %collective-permute-start.19 = (f32[8,16,512]{2,1,0:T(8,128)S(1)}, f32[8,16,512]{2,1,0:T(8,128)S(1)}, u32[]{:S(2)}, u32[]{:S(2)}) collective-permute-start(f32[8,16,512]{2,1,0:T(8,128)S(1)} %collective-permute-done.15), channel_id=1, source_target_pairs={{0,28},{4,0},{8,4},{12,8},{16,12},{20,16},{24,20},{28,24},{1,29},{... | collective-permute-start | bytes 786440 | tf_op jit(solution)/shard_map/ppermute | solution.py:26
  37.0 12.3 %collective-permute-start.18 = (f32[8,16,512]{2,1,0:T(8,128)S(1)}, f32[8,16,512]{2,1,0:T(8,128)S(1)}, u32[]{:S(2)}, u32[]{:S(2)}) collective-permute-start(f32[8,16,512]{2,1,0:T(8,128)S(1)} %collective-permute-done.14), channel_id=1, source_target_pairs={{0,4},{4,8},{8,12},{12,16},{16,20},{20,24},{24,28},{28,0},{1,5},{5... | collective-permute-start | bytes 786440 | tf_op jit(solution)/shard_map/ppermute | solution.py:26
  40.1 10.2 %collective-permute-start.22 = (f32[8,16,512]{2,1,0:T(8,128)S(1)}, f32[8,16,512]{2,1,0:T(8,128)S(1)}, u32[]{:S(2)}, u32[]{:S(2)}) collective-permute-start(f32[8,16,512]{2,1,0:T(8,128)S(1)} %collective-permute-done.16), channel_id=1, source_target_pairs={{0,4},{4,8},{8,12},{12,16},{16,20},{20,24},{24,28},{28,0},{1,5},{5... | collective-permute-start | bytes 786440 | tf_op jit(solution)/shard_map/ppermute | solution.py:26
  49.2 56.3 %collective-permute-start.20 = (f32[6,8,16,512]{3,2,1,0:T(8,128)S(1)}, f32[6,8,16,512]{3,2,1,0:T(8,128)S(1)}, u32[]{:S(2)}, u32[]{:S(2)}) collective-permute-start(f32[6,8,16,512]{3,2,1,0:T(8,128)S(1)} %bitcast_dynamic-update-slice_fusion.6.refs_0_), channel_id=1, source_target_pairs={{0,1},{1,0},{2,3},{3,2},{4,5},{5,4},{6,7},{7,6},{8,9},{9,8},{10,11... | collective-permute-start | bytes 4718600 | tf_op jit(solution)/shard_map/ppermute | solution.py:21
  50.3 11.0 %collective-permute-start.24 = (f32[8,16,512]{2,1,0:T(8,128)S(1)}, f32[8,16,512]{2,1,0:T(8,128)S(1)}, u32[]{:S(2)}, u32[]{:S(2)}) collective-permute-start(f32[8,16,512]{2,1,0:T(8,128)S(1)} %collective-permute-done.18), channel_id=1, source_target_pairs={{0,4},{4,8},{8,12},{12,16},{16,20},{20,24},{24,28},{28,0},{1,5},{5... | collective-permute-start | bytes 786440 | tf_op jit(solution)/shard_map/ppermute | solution.py:26
  54.6 10.3 %collective-permute-start.26 = (f32[8,16,512]{2,1,0:T(8,128)S(1)}, f32[8,16,512]{2,1,0:T(8,128)S(1)}, u32[]{:S(2)}, u32[]{:S(2)}) collective-permute-start(f32[8,16,512]{2,1,0:T(8,128)S(1)} %collective-permute-done.22), channel_id=1, source_target_pairs={{0,4},{4,8},{8,12},{12,16},{16,20},{20,24},{24,28},{28,0},{1,5},{5... | collective-permute-start | bytes 786440 | tf_op jit(solution)/shard_map/ppermute | solution.py:26
  65.2 43.8 %collective-permute-start.28 = (f32[6,8,16,512]{3,2,1,0:T(8,128)S(1)}, f32[6,8,16,512]{3,2,1,0:T(8,128)S(1)}, u32[]{:S(2)}, u32[]{:S(2)}) collective-permute-start(f32[6,8,16,512]{3,2,1,0:T(8,128)S(1)} %bitcast_dynamic-update-slice_fusion.refs_1_), channel_id=1, source_target_pairs={{0,1},{1,0},{2,3},{3,2},{4,5},{5,4},{6,7},{7,6},{8,9},{9,8},{10,11... | collective-permute-start | bytes 4718600 | tf_op jit(solution)/shard_map/ppermute | solution.py:21
  65.3 20.5 %collective-permute-start.4 = (f32[3,8,32,256]{3,2,1,0:T(8,128)S(1)}, f32[3,8,32,256]{3,2,1,0:T(8,128)S(1)}, u32[]{:S(2)}, u32[]{:S(2)}) collective-permute-start(f32[3,8,32,256]{3,2,1,0:T(8,128)S(1)} %pad_maximum_fusion.1.refs_1_), channel_id=1, source_target_pairs={{0,2},{2,0},{32,34},{34,32},{1,3},{3,1},{33,35},{35,33},{4,6},{6,4... | collective-permute-start | bytes 2359304 | tf_op jit(solution)/shard_map/ppermute | solution.py:21
  76.0 29.5 %collective-permute-start.21 = (f32[4,8,16,512]{3,2,1,0:T(8,128)S(1)}, f32[4,8,16,512]{3,2,1,0:T(8,128)S(1)}, u32[]{:S(2)}, u32[]{:S(2)}) collective-permute-start(f32[4,8,16,512]{3,2,1,0:T(8,128)S(1)} %pad_maximum_fusion.refs_1_.refs_0_), channel_id=1, source_target_pairs={{0,1},{1,0},{2,3},{3,2},{4,5},{5,4},{6,7},{7,6},{8,9},{9,8},{10,11... | collective-permute-start | bytes 3145736 | tf_op jit(solution)/shard_map/ppermute | solution.py:21
  76.0 15.4 %collective-permute-start.3 = (f32[8,32,256]{2,1,0:T(8,128)S(1)}, f32[8,32,256]{2,1,0:T(8,128)S(1)}, u32[]{:S(2)}, u32[]{:S(2)}) collective-permute-start(f32[8,32,256]{2,1,0:T(8,128)S(1)} %get-tuple-element.53), channel_id=1, source_target_pairs={{0,2},{2,0},{32,34},{34,32},{1,3},{3,1},{33,35},{35,33},{4,6},{6,4... | collective-permute-start | bytes 786440 | tf_op jit(solution)/shard_map/ppermute | solution.py:21
  85.8 16.3 %collective-permute-start.7 = (f32[2,8,32,256]{3,2,1,0:T(8,128)S(1)}, f32[2,8,32,256]{3,2,1,0:T(8,128)S(1)}, u32[]{:S(2)}, u32[]{:S(2)}) collective-permute-start(f32[2,8,32,256]{3,2,1,0:T(8,128)S(1)} %pad_maximum_fusion.2), channel_id=1, source_target_pairs={{0,2},{2,0},{32,34},{34,32},{1,3},{3,1},{33,35},{35,33},{4,6},{6,4... | collective-permute-start | bytes 1572872 | tf_op jit(solution)/shard_map/ppermute | solution.py:21
  91.4 13.7 %collective-permute-start.8 = (f32[2,8,32,256]{3,2,1,0:T(8,128)S(1)}, f32[2,8,32,256]{3,2,1,0:T(8,128)S(1)}, u32[]{:S(2)}, u32[]{:S(2)}) collective-permute-start(f32[2,8,32,256]{3,2,1,0:T(8,128)S(1)} %slice.57), channel_id=1, source_target_pairs={{0,34},{2,32},{32,2},{34,0},{1,35},{3,33},{33,3},{35,1},{4,38},{6,... | collective-permute-start | bytes 1572872 | tf_op jit(solution)/shard_map/ppermute | solution.py:21
  111.6 12.2 %collective-permute-start.35 = (f32[2,4,32,256]{3,2,1,0:T(8,128)S(1)}, f32[2,4,32,256]{3,2,1,0:T(8,128)S(1)}, u32[]{:S(2)}, u32[]{:S(2)}) collective-permute-start(f32[2,4,32,256]{3,2,1,0:T(8,128)S(1)} %get-tuple-element.51), channel_id=1, source_target_pairs={{0,192},{64,128},{128,64},{192,0},{1,193},{65,129},{129,65},{193,1... | collective-permute-start | bytes 786440 | tf_op jit(solution)/shard_map/ppermute | solution.py:21
  119.8 12.0 %collective-permute-start.29 = (f32[2,4,32,256]{3,2,1,0:T(8,128)S(1)}, f32[2,4,32,256]{3,2,1,0:T(8,128)S(1)}, u32[]{:S(2)}, u32[]{:S(2)}) collective-permute-start(f32[2,4,32,256]{3,2,1,0:T(8,128)S(1)} %get-tuple-element.42), channel_id=1, source_target_pairs={{0,64},{64,0},{128,192},{192,128},{1,65},{65,1},{129,193},{193,129... | collective-permute-start | bytes 786440 | tf_op jit(solution)/shard_map/ppermute | solution.py:21
  123.8 10.0 %collective-permute-start.36 = (f32[4,32,256]{2,1,0:T(8,128)S(1)}, f32[4,32,256]{2,1,0:T(8,128)S(1)}, u32[]{:S(2)}, u32[]{:S(2)}) collective-permute-start(f32[4,32,256]{2,1,0:T(8,128)S(1)} %fusion.42), channel_id=1, source_target_pairs={{0,64},{64,0},{128,192},{192,128},{1,65},{65,1},{129,193},{193,129... | collective-permute-start | bytes 393224 | tf_op jit(solution)/shard_map/ppermute | solution.py:21
  (17 other events, 125.6 us)

commit v2 on v1

--- a/solution.py
+++ b/solution.py
@@ -24,12 +24,6 @@
 def shift(v, axis, step):
     n = lax.axis_size(axis)
     return lax.ppermute(v, axis, [(i, (i + step) % n) for i in range(n)])
-
-
-def pick(pieces, index):
-    low = jnp.where(index % 2 == 1, pieces[1], pieces[0])
-    high = jnp.where(index % 2 == 1, pieces[3], pieces[2])
-    return jnp.where(index >= 2, high, low)
 
 
 def lane_order(z, c):
@@ -70,8 +64,29 @@
         in_specs=[VMEM],
         out_specs=(VMEM,) * 4,
         compiler_params=PARAMS,
+        cost_estimate=pl.CostEstimate(flops=1<<31, bytes_accessed=1<<23, transcendentals=0),
         name="cut_right",
     )(b)
+
+
+def place(got):
+    def kernel(*refs):
+        y = column_group()
+        for h in range(2):
+            for c in range(4):
+                d = jnp.bitwise_xor(y, 2 * h + c // 2)
+                at = pl.ds(512 * (c % 2), 512)
+                low = jnp.where(d % 2 == 1, refs[1][:, at], refs[0][:, at])
+                high = jnp.where(d % 2 == 1, refs[3][:, at], refs[2][:, at])
+                refs[4][:, :, h, c, :] = jnp.where(d >= 2, high, low).reshape(8, 4, 512)
+
+    return pl.pallas_call(
+        kernel,
+        out_shape=jax.ShapeDtypeStruct((8, 4, 2, 4, 512), F32),
+        in_specs=[VMEM] * 4,
+        compiler_params=PARAMS,
+        name="place",
+    )(*got)
 
 
 def join_right(got):
@@ -124,6 +139,39 @@
     )(*left)
 
 
+def split_far(one, low, high):
+    def kernel(one_ref, low_ref, high_ref, *outs):
+        def step(b, carry):
+            blocks = one_ref[b], low_ref[b], high_ref[b + 4]
+            for row, block in zip((0, 32, 96), blocks):
+                put(outs, row, b, block)
+            return carry
+
+        def put(outs, row, b, block):
+            for phase in range(2):
+                high, low = parts(block[:, 128 * phase : 128 * phase + 128])
+                for k3, v in enumerate((high, high, low)):
+                    at = pl.ds(pl.multiple_of(1024 * k3 + b * 128, 128), 128)
+                    outs[phase][pl.ds(row, 32), at] = v
+
+        def middle(b, carry):
+            put(outs, 64, b, low_ref[b + 8])
+            put(outs, 64, b + 4, high_ref[b])
+            return carry
+
+        lax.fori_loop(0, 8, step, 0)
+        lax.fori_loop(0, 4, middle, 0)
+
+    return pl.pallas_call(
+        kernel,
+        out_shape=(jax.ShapeDtypeStruct((128, 3072), BF16),) * 2,
+        in_specs=[VMEM] * 3,
+        out_specs=(VMEM,) * 2,
+        compiler_params=PARAMS,
+        name="split_far",
+    )(one, low, high)
+
+
 def sources(blocks):
     arrays = []
     for v, _ in blocks:
@@ -220,7 +268,6 @@
 
 def placed_product(a, b):
     x, z, c = lax.axis_index("x"), lax.axis_index("z"), lax.axis_index("c")
-    y = lax.axis_index(Y)
 
     b_for = cut_right(b)
     b_got = [b_for[0]] + [swap(b_for[d], Y, d) for d in (1, 2, 3)]
@@ -233,10 +280,11 @@
     one, rest = a_got[0], jnp.stack(a_got[1:])
     near1 = swap(one, Y, 1), swap(rest, Y, 1)
     near3 = swap(one, Y, 3), swap(rest, Y, 3)
-    far_low = swap(jnp.stack([near3[0], near3[1][0]]), Y, 1)
-    far_high = swap(near1[1][1:], Y, 3)
+    far = [
+        swap(one, Y, 2), swap(near3[1].reshape(24, 32, 256)[:12], Y, 1), swap(near1[1].reshape(24, 32, 256)[12:], Y, 3)
+    ]
     near = split_left([one[None], rest, near1[0][None], near1[1], near3[0][None], near3[1]])
-    far = split_left([far_low, far_high])
+    far = split_far(*far)
 
     own, other = [{}, {}], [{}, {}]
     up, down, held = list(halves), list(halves), list(halves)
@@ -274,8 +322,7 @@
             sums.append(keep + got[0] + swap(pass_on + got[1], "x", second))
     summed = jnp.concatenate(sums, axis=2)
     back = [summed[0]] + [swap(summed[d], Y, d) for d in (1, 2, 3)]
-    placed = jnp.stack([pick(back, y ^ k) for k in range(4)], axis=1)
-    return placed.reshape(8, 4, 2, 4, 512)
+    return place(back)
 
 
 def solution(mesh):

time: 151 us -> 158 us (1.046)
  starting transfers between devices: 59.7 us -> 64.1 us
  waiting for transfers between devices: 72.8 us -> 76.3 us
  local copies, waits for them, and re-layouts: 4.95 us -> 2.24 us
    ppermute x26 -> x27, starting transfers between devices: 33.3 us -> 39.2 us  [swap(): return lax.ppermute(v, axis, [(i, i ^ bits) for i in range(n)])]
    ppermute x26 -> x27, waiting for transfers between devices: 52.9 us -> 56.4 us  [swap(): return lax.ppermute(v, axis, [(i, i ^ bits) for i in range(n)])]
  transfers between devices with their start and end apart: 40 -> 41, of which waited for: 24 -> 25; matrix products, arithmetic and copies ran while one was open for 3% -> 2% of each run, Pallas kernels for 5% -> 5%
where the time goes in v2:
time: 158 us; the launch traced here: 157 us
  waiting for transfers between devices  76.3 us (48%)
  starting transfers between devices  64.1 us (41%)
  Pallas kernels  11.8 us (7%)
  local copies, waits for them, and re-layouts  2.24 us (1%)
    ppermute x27, waiting for transfers between devices, swap(): return lax.ppermute(v, axis, [(i, i ^ bits) for i in range(n)])  56.4 us
    ppermute x27, starting transfers between devices, swap(): return lax.ppermute(v, axis, [(i, i ^ bits) for i in range(n)])  39.2 us
    ppermute x14, starting transfers between devices, shift(): return lax.ppermute(v, axis, [(i, (i + step) % n) for i in range(n)])  25 us
    ppermute x14, waiting for transfers between devices, shift(): return lax.ppermute(v, axis, [(i, (i + step) % n) for i in range(n)])  19.9 us
    pallas_call x2, Pallas kernels, late_product(): pl.pallas_call(kernel, out_shape=(one, one, two) * 2, in_specs=[VMEM] * (...  5.13 us
    pallas_call x1, Pallas kernels, early_product(): pl.pallas_call(kernel, out_shape=(jax.ShapeDtypeStruct((384, 1024), F32),...  3.43 us
  transfers between devices with their start and end apart: 41, of which 25 were waited for; matrix products, arithmetic and copies ran while one was open for 2% of the time, Pallas kernels for 5%

profile of v2, /device:TPU:8, one launch (start us, length us, event | category | flops | bytes accessed | tf_op | source)
XLA Modules:
  0.0 156.6 jit_solution(9824314521429005622)
XLA Ops:
  1.2 2.2 %collective-permute-start.10 = (f32[8,4,1024]{2,1,0:T(4,128)S(1)}, f32[8,4,1024]{2,1,0:T(4,128)S(1)}, u32[]{:S(2)}, u32[]{:S(2)}) collective-permute-start(f32[8,4,1024]{2,1,0:T(4,128)S(1)} %get-tuple-element.34), channel_id=1, source_target_pairs={{0,2},{2,0},{32,34},{34,32},{1,3},{3,1},{33,35},{35,33},{4,6},{6,4... | collective-permute-start | bytes 393224 | tf_op jit(solution)/shard_map/ppermute | solution.py:21
  7.4 2.6 %collective-permute-start.2 = (f32[8,32,256]{2,1,0:T(8,128)S(1)}, f32[8,32,256]{2,1,0:T(8,128)S(1)}, u32[]{:S(2)}, u32[]{:S(2)}) collective-permute-start(f32[8,32,256]{2,1,0:T(8,128)S(1)} %get-tuple-element.57), channel_id=1, source_target_pairs={{0,192},{64,128},{128,64},{192,0},{1,193},{65,129},{129,65},{193,1... | collective-permute-start | bytes 786440 | tf_op jit(solution)/shard_map/ppermute | solution.py:21
  14.0 4.0 %collective-permute-start.14 = (f32[8,16,512]{2,1,0:T(8,128)S(1)}, f32[8,16,512]{2,1,0:T(8,128)S(1)}, u32[]{:S(2)}, u32[]{:S(2)}) collective-permute-start(f32[8,16,512]{2,1,0:T(8,128)S(1)} %get-tuple-element.37), channel_id=1, source_target_pairs={{0,28},{4,0},{8,4},{12,8},{16,12},{20,16},{24,20},{28,24},{1,29},{... | collective-permute-start | bytes 786440 | tf_op jit(solution)/shard_map/ppermute | solution.py:26
  18.0 3.2 %collective-permute-start.16 = (f32[8,16,512]{2,1,0:T(8,128)S(1)}, f32[8,16,512]{2,1,0:T(8,128)S(1)}, u32[]{:S(2)}, u32[]{:S(2)}) collective-permute-start(f32[8,16,512]{2,1,0:T(8,128)S(1)} %get-tuple-element.38), channel_id=1, source_target_pairs={{0,28},{4,0},{8,4},{12,8},{16,12},{20,16},{24,20},{28,24},{1,29},{... | collective-permute-start | bytes 786440 | tf_op jit(solution)/shard_map/ppermute | solution.py:26
  21.3 3.8 %collective-permute-done.13 = f32[8,16,512]{2,1,0:T(8,128)S(1)} collective-permute-done((f32[8,16,512]{2,1,0:T(8,128)S(1)}, f32[8,16,512]{2,1,0:T(8,128)S(1)}, u32[]{:S(2)}, u32[]{:S(2)}) %collective-permute-start.13) | collective-permute-done | bytes 262176 | tf_op jit(solution)/shard_map/ppermute | solution.py:26
  25.1 3.3 %collective-permute-start.18 = (f32[8,16,512]{2,1,0:T(8,128)S(1)}, f32[8,16,512]{2,1,0:T(8,128)S(1)}, u32[]{:S(2)}, u32[]{:S(2)}) collective-permute-start(f32[8,16,512]{2,1,0:T(8,128)S(1)} %collective-permute-done.14), channel_id=1, source_target_pairs={{0,28},{4,0},{8,4},{12,8},{16,12},{20,16},{24,20},{28,24},{1,29},{... | collective-permute-start | bytes 786440 | tf_op jit(solution)/shard_map/ppermute | solution.py:26
  30.3 3.7 %collective-permute-start.20 = (f32[8,16,512]{2,1,0:T(8,128)S(1)}, f32[8,16,512]{2,1,0:T(8,128)S(1)}, u32[]{:S(2)}, u32[]{:S(2)}) collective-permute-start(f32[8,16,512]{2,1,0:T(8,128)S(1)} %collective-permute-done.16), channel_id=1, source_target_pairs={{0,28},{4,0},{8,4},{12,8},{16,12},{20,16},{24,20},{28,24},{1,29},{... | collective-permute-start | bytes 786440 | tf_op jit(solution)/shard_map/ppermute | solution.py:26
  36.0 3.7 %collective-permute-start.24 = (f32[8,16,512]{2,1,0:T(8,128)S(1)}, f32[8,16,512]{2,1,0:T(8,128)S(1)}, u32[]{:S(2)}, u32[]{:S(2)}) collective-permute-start(f32[8,16,512]{2,1,0:T(8,128)S(1)} %collective-permute-done.18), channel_id=1, source_target_pairs={{0,28},{4,0},{8,4},{12,8},{16,12},{20,16},{24,20},{28,24},{1,29},{... | collective-permute-start | bytes 786440 | tf_op jit(solution)/shard_map/ppermute | solution.py:26
  41.6 3.0 %collective-permute-start.1 = (f32[8,32,256]{2,1,0:T(8,128)S(1)}, f32[8,32,256]{2,1,0:T(8,128)S(1)}, u32[]{:S(2)}, u32[]{:S(2)}) collective-permute-start(f32[8,32,256]{2,1,0:T(8,128)S(1)} %get-tuple-element.54), channel_id=1, source_target_pairs={{0,128},{64,192},{128,0},{192,64},{1,129},{65,193},{129,1},{193,65... | collective-permute-start | bytes 786440 | tf_op jit(solution)/shard_map/ppermute | solution.py:21
  48.4 2.5 %collective-permute-start = (f32[8,32,256]{2,1,0:T(8,128)S(1)}, f32[8,32,256]{2,1,0:T(8,128)S(1)}, u32[]{:S(2)}, u32[]{:S(2)}) collective-permute-start(f32[8,32,256]{2,1,0:T(8,128)S(1)} %get-tuple-element.55), channel_id=1, source_target_pairs={{0,64},{64,0},{128,192},{192,128},{1,65},{65,1},{129,193},{193,129... | collective-permute-start | bytes 786440 | tf_op jit(solution)/shard_map/ppermute | solution.py:21
  56.1 4.3 %collective-permute-done.27 = f32[8,16,512]{2,1,0:T(8,128)S(1)} collective-permute-done((f32[8,16,512]{2,1,0:T(8,128)S(1)}, f32[8,16,512]{2,1,0:T(8,128)S(1)}, u32[]{:S(2)}, u32[]{:S(2)}) %collective-permute-start.27) | collective-permute-done | bytes 262176 | tf_op jit(solution)/shard_map/ppermute | solution.py:26
  62.8 2.2 %collective-permute-start.4 = (f32[3,8,32,256]{3,2,1,0:T(8,128)S(1)}, f32[3,8,32,256]{3,2,1,0:T(8,128)S(1)}, u32[]{:S(2)}, u32[]{:S(2)}) collective-permute-start(f32[3,8,32,256]{3,2,1,0:T(8,128)S(1)} %pad_maximum_fusion.1.refs_1_), channel_id=1, source_target_pairs={{0,2},{2,0},{32,34},{34,32},{1,3},{3,1},{33,35},{35,33},{4,6},{6,4... | collective-permute-start | bytes 2359304 | tf_op jit(solution)/shard_map/ppermute | solution.py:21
  65.7 23.2 %collective-permute-done.3 = f32[8,32,256]{2,1,0:T(8,128)S(1)} collective-permute-done((f32[8,32,256]{2,1,0:T(8,128)S(1)}, f32[8,32,256]{2,1,0:T(8,128)S(1)}, u32[]{:S(2)}, u32[]{:S(2)}) %collective-permute-start.3) | collective-permute-done | bytes 262176 | tf_op jit(solution)/shard_map/ppermute | solution.py:21
  88.9 3.8 %collective-permute-start.7 = (f32[8,32,256]{2,1,0:T(8,128)S(1)}, f32[8,32,256]{2,1,0:T(8,128)S(1)}, u32[]{:S(2)}, u32[]{:S(2)}) collective-permute-start(f32[8,32,256]{2,1,0:T(8,128)S(1)} %get-tuple-element.53), channel_id=1, source_target_pairs={{0,32},{2,34},{32,0},{34,2},{1,33},{3,35},{33,1},{35,3},{4,36},{6,... | collective-permute-start | bytes 786440 | tf_op jit(solution)/shard_map/ppermute | solution.py:21
  92.8 10.5 %collective-permute-done.5 = f32[8,32,256]{2,1,0:T(8,128)S(1)} collective-permute-done((f32[8,32,256]{2,1,0:T(8,128)S(1)}, f32[8,32,256]{2,1,0:T(8,128)S(1)}, u32[]{:S(2)}, u32[]{:S(2)}) %collective-permute-start.5) | collective-permute-done | bytes 262176 | tf_op jit(solution)/shard_map/ppermute | solution.py:21
  103.2 3.0 %collective-permute-start.8 = (f32[12,32,256]{2,1,0:T(8,128)S(1)}, f32[12,32,256]{2,1,0:T(8,128)S(1)}, u32[]{:S(2)}, u32[]{:S(2)}) collective-permute-start(f32[12,32,256]{2,1,0:T(8,128)S(1)} %slice.56), channel_id=1, source_target_pairs={{0,2},{2,0},{32,34},{34,32},{1,3},{3,1},{33,35},{35,33},{4,6},{6,4... | collective-permute-start | bytes 1179656 | tf_op jit(solution)/shard_map/ppermute | solution.py:21
  107.6 7.5 %collective-permute-done.8.low_ref = f32[12,32,256]{2,1,0:T(8,128)S(1)} collective-permute-done((f32[12,32,256]{2,1,0:T(8,128)S(1)}, f32[12,32,256]{2,1,0:T(8,128)S(1)}, u32[]{:S(2)}, u32[]{:S(2)}) %collective-permute-start.8) | collective-permute-done | bytes 393248 | tf_op jit(solution)/shard_map/ppermute | solution.py:21
  117.1 3.4 %early_product.1 = (f32[384,1024]{1,0:T(8,128)S(1)}, bf16[3072,1024]{1,0:T(8,128)(2,1)S(1)}) custom-call(bf16[384,3072]{1,0:T(8,128)(2,1)S(1)} %get-tuple-element.32.a, f32[6,8,16,512]{3,2,1,0:T(8,128)S(1)} %bitcast_dynamic-update-slice_fusion.6.refs_0_, f32[4,8,16,512]{3,2,1,0:T(8,128)S(1)} %pad_maximum_fusion.refs_1_.refs_0_, ...), custom_call_target="tpu_custom_call" | custom-call | tf_op jit(solution)/shard_map/early_product/pallas_call | solution.py:216
  120.5 2.6 %late_product.3 = (f32[4,32,256]{2,1,0:T(8,128)S(1)}, f32[4,32,256]{2,1,0:T(8,128)S(1)}, f32[2,4,32,256]{3,2,1,0:T(8,128)S(1)}, f32[4,32,256]{2,1,0:T(8,128)S(1)...) custom-call(bf16[384,3072]{1,0:T(8,128)(2,1)S(1)} %get-tuple-element.29.a, ...), custom_call_target="tpu_custom_call" | custom-call | tf_op jit(solution)/shard_map/late_product/pallas_call | solution.py:258
  123.1 3.8 %collective-permute-start.36 = (f32[2,4,32,256]{3,2,1,0:T(8,128)S(1)}, f32[2,4,32,256]{3,2,1,0:T(8,128)S(1)}, u32[]{:S(2)}, u32[]{:S(2)}) collective-permute-start(f32[2,4,32,256]{3,2,1,0:T(8,128)S(1)} %get-tuple-element.51), channel_id=1, source_target_pairs={{0,192},{64,128},{128,64},{192,0},{1,193},{65,129},{129,65},{193,1... | collective-permute-start | bytes 786440 | tf_op jit(solution)/shard_map/ppermute | solution.py:21
  128.0 2.6 %late_product.2 = (f32[4,32,256]{2,1,0:T(8,128)S(1)}, f32[4,32,256]{2,1,0:T(8,128)S(1)}, f32[2,4,32,256]{3,2,1,0:T(8,128)S(1)}, f32[4,32,256]{2,1,0:T(8,128)S(1)...) custom-call(bf16[384,3072]{1,0:T(8,128)(2,1)S(1)} %get-tuple-element.29.a, ...), custom_call_target="tpu_custom_call" | custom-call | tf_op jit(solution)/shard_map/late_product/pallas_call | solution.py:258
  134.8 3.2 %collective-permute-start.35 = (f32[4,32,256]{2,1,0:T(8,128)S(1)}, f32[4,32,256]{2,1,0:T(8,128)S(1)}, u32[]{:S(2)}, u32[]{:S(2)}) collective-permute-start(f32[4,32,256]{2,1,0:T(8,128)S(1)} %fusion.45), channel_id=1, source_target_pairs={{0,192},{64,128},{128,64},{192,0},{1,193},{65,129},{129,65},{193,1... | collective-permute-start | bytes 393224 | tf_op jit(solution)/shard_map/ppermute | solution.py:21
  144.6 2.3 %collective-permute-done.31 = f32[4,32,256]{2,1,0:T(8,128)S(1)} collective-permute-done((f32[4,32,256]{2,1,0:T(8,128)S(1)}, f32[4,32,256]{2,1,0:T(8,128)S(1)}, u32[]{:S(2)}, u32[]{:S(2)}) %collective-permute-start.31) | collective-permute-done | bytes 131104 | tf_op jit(solution)/shard_map/ppermute | solution.py:21
  152.0 3.1 %collective-permute-done.39.refs_2_ = f32[32,1024]{1,0:T(8,128)S(1)} collective-permute-done((f32[32,1024]{1,0:T(8,128)S(1)}, f32[32,1024]{1,0:T(8,128)S(1)}, u32[]{:S(2)}, u32[]{:S(2)}) %collective-permute-start.39) | collective-permute-done | bytes 131104 | tf_op jit(solution)/shard_map/ppermute | solution.py:21
  (107 shorter events, 48.7 us)
Async XLA Ops:
  7.4 55.3 %collective-permute-start.2 = (f32[8,32,256]{2,1,0:T(8,128)S(1)}, f32[8,32,256]{2,1,0:T(8,128)S(1)}, u32[]{:S(2)}, u32[]{:S(2)}) collective-permute-start(f32[8,32,256]{2,1,0:T(8,128)S(1)} %get-tuple-element.57), channel_id=1, source_target_pairs={{0,192},{64,128},{128,64},{192,0},{1,193},{65,129},{129,65},{193,1... | collective-permute-start | bytes 786440 | tf_op jit(solution)/shard_map/ppermute | solution.py:21
  12.0 13.1 %collective-permute-start.13 = (f32[8,16,512]{2,1,0:T(8,128)S(1)}, f32[8,16,512]{2,1,0:T(8,128)S(1)}, u32[]{:S(2)}, u32[]{:S(2)}) collective-permute-start(f32[8,16,512]{2,1,0:T(8,128)S(1)} %get-tuple-element.37), channel_id=1, source_target_pairs={{0,4},{4,8},{8,12},{12,16},{16,20},{20,24},{24,28},{28,0},{1,5},{5... | collective-permute-start | bytes 786440 | tf_op jit(solution)/shard_map/ppermute | solution.py:26
  14.0 11.1 %collective-permute-start.14 = (f32[8,16,512]{2,1,0:T(8,128)S(1)}, f32[8,16,512]{2,1,0:T(8,128)S(1)}, u32[]{:S(2)}, u32[]{:S(2)}) collective-permute-start(f32[8,16,512]{2,1,0:T(8,128)S(1)} %get-tuple-element.37), channel_id=1, source_target_pairs={{0,28},{4,0},{8,4},{12,8},{16,12},{20,16},{24,20},{28,24},{1,29},{... | collective-permute-start | bytes 786440 | tf_op jit(solution)/shard_map/ppermute | solution.py:26
  18.0 16.0 %collective-permute-start.15 = (f32[8,16,512]{2,1,0:T(8,128)S(1)}, f32[8,16,512]{2,1,0:T(8,128)S(1)}, u32[]{:S(2)}, u32[]{:S(2)}) collective-permute-start(f32[8,16,512]{2,1,0:T(8,128)S(1)} %get-tuple-element.38), channel_id=1, source_target_pairs={{0,4},{4,8},{8,12},{12,16},{16,20},{20,24},{24,28},{28,0},{1,5},{5... | collective-permute-start | bytes 786440 | tf_op jit(solution)/shard_map/ppermute | solution.py:26
  18.0 12.3 %collective-permute-start.16 = (f32[8,16,512]{2,1,0:T(8,128)S(1)}, f32[8,16,512]{2,1,0:T(8,128)S(1)}, u32[]{:S(2)}, u32[]{:S(2)}) collective-permute-start(f32[8,16,512]{2,1,0:T(8,128)S(1)} %get-tuple-element.38), channel_id=1, source_target_pairs={{0,28},{4,0},{8,4},{12,8},{16,12},{20,16},{24,20},{28,24},{1,29},{... | collective-permute-start | bytes 786440 | tf_op jit(solution)/shard_map/ppermute | solution.py:26
  25.1 10.4 %collective-permute-start.17 = (f32[8,16,512]{2,1,0:T(8,128)S(1)}, f32[8,16,512]{2,1,0:T(8,128)S(1)}, u32[]{:S(2)}, u32[]{:S(2)}) collective-permute-start(f32[8,16,512]{2,1,0:T(8,128)S(1)} %collective-permute-done.13), channel_id=1, source_target_pairs={{0,4},{4,8},{8,12},{12,16},{16,20},{20,24},{24,28},{28,0},{1,5},{5... | collective-permute-start | bytes 786440 | tf_op jit(solution)/shard_map/ppermute | solution.py:26
  25.1 10.9 %collective-permute-start.18 = (f32[8,16,512]{2,1,0:T(8,128)S(1)}, f32[8,16,512]{2,1,0:T(8,128)S(1)}, u32[]{:S(2)}, u32[]{:S(2)}) collective-permute-start(f32[8,16,512]{2,1,0:T(8,128)S(1)} %collective-permute-done.14), channel_id=1, source_target_pairs={{0,28},{4,0},{8,4},{12,8},{16,12},{20,16},{24,20},{28,24},{1,29},{... | collective-permute-start | bytes 786440 | tf_op jit(solution)/shard_map/ppermute | solution.py:26
  30.3 11.2 %collective-permute-start.20 = (f32[8,16,512]{2,1,0:T(8,128)S(1)}, f32[8,16,512]{2,1,0:T(8,128)S(1)}, u32[]{:S(2)}, u32[]{:S(2)}) collective-permute-start(f32[8,16,512]{2,1,0:T(8,128)S(1)} %collective-permute-done.16), channel_id=1, source_target_pairs={{0,28},{4,0},{8,4},{12,8},{16,12},{20,16},{24,20},{28,24},{1,29},{... | collective-permute-start | bytes 786440 | tf_op jit(solution)/shard_map/ppermute | solution.py:26
  34.0 10.6 %collective-permute-start.19 = (f32[8,16,512]{2,1,0:T(8,128)S(1)}, f32[8,16,512]{2,1,0:T(8,128)S(1)}, u32[]{:S(2)}, u32[]{:S(2)}) collective-permute-start(f32[8,16,512]{2,1,0:T(8,128)S(1)} %collective-permute-done.15), channel_id=1, source_target_pairs={{0,4},{4,8},{8,12},{12,16},{16,20},{20,24},{24,28},{28,0},{1,5},{5... | collective-permute-start | bytes 786440 | tf_op jit(solution)/shard_map/ppermute | solution.py:26
  35.5 11.2 %collective-permute-start.23 = (f32[8,16,512]{2,1,0:T(8,128)S(1)}, f32[8,16,512]{2,1,0:T(8,128)S(1)}, u32[]{:S(2)}, u32[]{:S(2)}) collective-permute-start(f32[8,16,512]{2,1,0:T(8,128)S(1)} %collective-permute-done.17), channel_id=1, source_target_pairs={{0,4},{4,8},{8,12},{12,16},{16,20},{20,24},{24,28},{28,0},{1,5},{5... | collective-permute-start | bytes 786440 | tf_op jit(solution)/shard_map/ppermute | solution.py:26
  36.0 12.5 %collective-permute-start.24 = (f32[8,16,512]{2,1,0:T(8,128)S(1)}, f32[8,16,512]{2,1,0:T(8,128)S(1)}, u32[]{:S(2)}, u32[]{:S(2)}) collective-permute-start(f32[8,16,512]{2,1,0:T(8,128)S(1)} %collective-permute-done.18), channel_id=1, source_target_pairs={{0,28},{4,0},{8,4},{12,8},{16,12},{20,16},{24,20},{28,24},{1,29},{... | collective-permute-start | bytes 786440 | tf_op jit(solution)/shard_map/ppermute | solution.py:26
  41.6 21.2 %collective-permute-start.1 = (f32[8,32,256]{2,1,0:T(8,128)S(1)}, f32[8,32,256]{2,1,0:T(8,128)S(1)}, u32[]{:S(2)}, u32[]{:S(2)}) collective-permute-start(f32[8,32,256]{2,1,0:T(8,128)S(1)} %get-tuple-element.54), channel_id=1, source_target_pairs={{0,128},{64,192},{128,0},{192,64},{1,129},{65,193},{129,1},{193,65... | collective-permute-start | bytes 786440 | tf_op jit(solution)/shard_map/ppermute | solution.py:21
  48.4 14.3 %collective-permute-start = (f32[8,32,256]{2,1,0:T(8,128)S(1)}, f32[8,32,256]{2,1,0:T(8,128)S(1)}, u32[]{:S(2)}, u32[]{:S(2)}) collective-permute-start(f32[8,32,256]{2,1,0:T(8,128)S(1)} %get-tuple-element.55), channel_id=1, source_target_pairs={{0,64},{64,0},{128,192},{192,128},{1,65},{65,1},{129,193},{193,129... | collective-permute-start | bytes 786440 | tf_op jit(solution)/shard_map/ppermute | solution.py:21
  60.4 56.6 %collective-permute-start.21 = (f32[6,8,16,512]{3,2,1,0:T(8,128)S(1)}, f32[6,8,16,512]{3,2,1,0:T(8,128)S(1)}, u32[]{:S(2)}, u32[]{:S(2)}) collective-permute-start(f32[6,8,16,512]{3,2,1,0:T(8,128)S(1)} %bitcast_dynamic-update-slice_fusion.6.refs_0_), channel_id=1, source_target_pairs={{0,1},{1,0},{2,3},{3,2},{4,5},{5,4},{6,7},{7,6},{8,9},{9,8},{10,11... | collective-permute-start | bytes 4718600 | tf_op jit(solution)/shard_map/ppermute | solution.py:21
  62.6 57.9 %collective-permute-start.29 = (f32[6,8,16,512]{3,2,1,0:T(8,128)S(1)}, f32[6,8,16,512]{3,2,1,0:T(8,128)S(1)}, u32[]{:S(2)}, u32[]{:S(2)}) collective-permute-start(f32[6,8,16,512]{3,2,1,0:T(8,128)S(1)} %bitcast_dynamic-update-slice_fusion.refs_1_), channel_id=1, source_target_pairs={{0,1},{1,0},{2,3},{3,2},{4,5},{5,4},{6,7},{7,6},{8,9},{9,8},{10,11... | collective-permute-start | bytes 4718600 | tf_op jit(solution)/shard_map/ppermute | solution.py:21
  62.8 26.0 %collective-permute-start.4 = (f32[3,8,32,256]{3,2,1,0:T(8,128)S(1)}, f32[3,8,32,256]{3,2,1,0:T(8,128)S(1)}, u32[]{:S(2)}, u32[]{:S(2)}) collective-permute-start(f32[3,8,32,256]{3,2,1,0:T(8,128)S(1)} %pad_maximum_fusion.1.refs_1_), channel_id=1, source_target_pairs={{0,2},{2,0},{32,34},{34,32},{1,3},{3,1},{33,35},{35,33},{4,6},{6,4... | collective-permute-start | bytes 2359304 | tf_op jit(solution)/shard_map/ppermute | solution.py:21
  65.1 23.8 %collective-permute-start.6 = (f32[3,8,32,256]{3,2,1,0:T(8,128)S(1)}, f32[3,8,32,256]{3,2,1,0:T(8,128)S(1)}, u32[]{:S(2)}, u32[]{:S(2)}) collective-permute-start(f32[3,8,32,256]{3,2,1,0:T(8,128)S(1)} %pad_maximum_fusion.1.refs_1_), channel_id=1, source_target_pairs={{0,34},{2,32},{32,2},{34,0},{1,35},{3,33},{33,3},{35,1},{4,38},{6,... | collective-permute-start | bytes 2359304 | tf_op jit(solution)/shard_map/ppermute | solution.py:21
  65.1 23.8 %collective-permute-start.3 = (f32[8,32,256]{2,1,0:T(8,128)S(1)}, f32[8,32,256]{2,1,0:T(8,128)S(1)}, u32[]{:S(2)}, u32[]{:S(2)}) collective-permute-start(f32[8,32,256]{2,1,0:T(8,128)S(1)} %get-tuple-element.53), channel_id=1, source_target_pairs={{0,2},{2,0},{32,34},{34,32},{1,3},{3,1},{33,35},{35,33},{4,6},{6,4... | collective-permute-start | bytes 786440 | tf_op jit(solution)/shard_map/ppermute | solution.py:21
  88.9 28.1 %collective-permute-start.22 = (f32[4,8,16,512]{3,2,1,0:T(8,128)S(1)}, f32[4,8,16,512]{3,2,1,0:T(8,128)S(1)}, u32[]{:S(2)}, u32[]{:S(2)}) collective-permute-start(f32[4,8,16,512]{3,2,1,0:T(8,128)S(1)} %pad_maximum_fusion.refs_1_.refs_0_), channel_id=1, source_target_pairs={{0,1},{1,0},{2,3},{3,2},{4,5},{5,4},{6,7},{7,6},{8,9},{9,8},{10,11... | collective-permute-start | bytes 3145736 | tf_op jit(solution)/shard_map/ppermute | solution.py:21
  88.9 14.3 %collective-permute-start.5 = (f32[8,32,256]{2,1,0:T(8,128)S(1)}, f32[8,32,256]{2,1,0:T(8,128)S(1)}, u32[]{:S(2)}, u32[]{:S(2)}) collective-permute-start(f32[8,32,256]{2,1,0:T(8,128)S(1)} %get-tuple-element.53), channel_id=1, source_target_pairs={{0,34},{2,32},{32,2},{34,0},{1,35},{3,33},{33,3},{35,1},{4,38},{6,... | collective-permute-start | bytes 786440 | tf_op jit(solution)/shard_map/ppermute | solution.py:21
  88.9 17.3 %collective-permute-start.7 = (f32[8,32,256]{2,1,0:T(8,128)S(1)}, f32[8,32,256]{2,1,0:T(8,128)S(1)}, u32[]{:S(2)}, u32[]{:S(2)}) collective-permute-start(f32[8,32,256]{2,1,0:T(8,128)S(1)} %get-tuple-element.53), channel_id=1, source_target_pairs={{0,32},{2,34},{32,0},{34,2},{1,33},{3,35},{33,1},{35,3},{4,36},{6,... | collective-permute-start | bytes 786440 | tf_op jit(solution)/shard_map/ppermute | solution.py:21
  103.2 11.9 %collective-permute-start.8 = (f32[12,32,256]{2,1,0:T(8,128)S(1)}, f32[12,32,256]{2,1,0:T(8,128)S(1)}, u32[]{:S(2)}, u32[]{:S(2)}) collective-permute-start(f32[12,32,256]{2,1,0:T(8,128)S(1)} %slice.56), channel_id=1, source_target_pairs={{0,2},{2,0},{32,34},{34,32},{1,3},{3,1},{33,35},{35,33},{4,6},{6,4... | collective-permute-start | bytes 1179656 | tf_op jit(solution)/shard_map/ppermute | solution.py:21
  106.2 10.4 %collective-permute-start.9 = (f32[12,32,256]{2,1,0:T(8,128)S(1)}, f32[12,32,256]{2,1,0:T(8,128)S(1)}, u32[]{:S(2)}, u32[]{:S(2)}) collective-permute-start(f32[12,32,256]{2,1,0:T(8,128)S(1)} %slice.57), channel_id=1, source_target_pairs={{0,34},{2,32},{32,2},{34,0},{1,35},{3,33},{33,3},{35,1},{4,38},{6,... | collective-permute-start | bytes 1179656 | tf_op jit(solution)/shard_map/ppermute | solution.py:21
  132.5 10.6 %collective-permute-start.37 = (f32[4,32,256]{2,1,0:T(8,128)S(1)}, f32[4,32,256]{2,1,0:T(8,128)S(1)}, u32[]{:S(2)}, u32[]{:S(2)}) collective-permute-start(f32[4,32,256]{2,1,0:T(8,128)S(1)} %fusion.42), channel_id=1, source_target_pairs={{0,64},{64,0},{128,192},{192,128},{1,65},{65,1},{129,193},{193,129... | collective-permute-start | bytes 393224 | tf_op jit(solution)/shard_map/ppermute | solution.py:21
  (19 other events, 133.3 us)

commit v3 on v1

--- a/solution.py
+++ b/solution.py
@@ -24,12 +24,6 @@
 def shift(v, axis, step):
     n = lax.axis_size(axis)
     return lax.ppermute(v, axis, [(i, (i + step) % n) for i in range(n)])
-
-
-def pick(pieces, index):
-    low = jnp.where(index % 2 == 1, pieces[1], pieces[0])
-    high = jnp.where(index % 2 == 1, pieces[3], pieces[2])
-    return jnp.where(index >= 2, high, low)
 
 
 def lane_order(z, c):
@@ -70,8 +64,29 @@
         in_specs=[VMEM],
         out_specs=(VMEM,) * 4,
         compiler_params=PARAMS,
+        cost_estimate=pl.CostEstimate(flops=1<<31, bytes_accessed=1<<23, transcendentals=0),
         name="cut_right",
     )(b)
+
+
+def place(got):
+    def kernel(*refs):
+        y = column_group()
+        for h in range(2):
+            for c in range(4):
+                d = jnp.bitwise_xor(y, 2 * h + c // 2)
+                at = pl.ds(512 * (c % 2), 512)
+                low = jnp.where(d % 2 == 1, refs[1][:, at], refs[0][:, at])
+                high = jnp.where(d % 2 == 1, refs[3][:, at], refs[2][:, at])
+                refs[4][:, :, h, c, :] = jnp.where(d >= 2, high, low).reshape(8, 4, 512)
+
+    return pl.pallas_call(
+        kernel,
+        out_shape=jax.ShapeDtypeStruct((8, 4, 2, 4, 512), F32),
+        in_specs=[VMEM] * 4,
+        compiler_params=PARAMS,
+        name="place",
+    )(*got)
 
 
 def join_right(got):
@@ -220,7 +235,6 @@
 
 def placed_product(a, b):
     x, z, c = lax.axis_index("x"), lax.axis_index("z"), lax.axis_index("c")
-    y = lax.axis_index(Y)
 
     b_for = cut_right(b)
     b_got = [b_for[0]] + [swap(b_for[d], Y, d) for d in (1, 2, 3)]
@@ -274,8 +288,7 @@
             sums.append(keep + got[0] + swap(pass_on + got[1], "x", second))
     summed = jnp.concatenate(sums, axis=2)
     back = [summed[0]] + [swap(summed[d], Y, d) for d in (1, 2, 3)]
-    placed = jnp.stack([pick(back, y ^ k) for k in range(4)], axis=1)
-    return placed.reshape(8, 4, 2, 4, 512)
+    return place(back)
 
 
 def solution(mesh):

time: 151 us -> 150 us (level); the launches traced: 151 us -> 148 us
  local copies, waits for them, and re-layouts: 4.95 us -> 2.25 us
  transfers between devices with their start and end apart: 40 -> 40, of which waited for: 24 -> 25; matrix products, arithmetic and copies ran while one was open for 3% -> 2% of each run, Pallas kernels for 5% -> 5%
where the time goes in v3:
time: 150 us; the launch traced here: 148 us
  waiting for transfers between devices  71.7 us (48%)
  starting transfers between devices  59.9 us (40%)
  Pallas kernels  11.7 us (8%)
  local copies, waits for them, and re-layouts  2.25 us (2%)
    ppermute x26, waiting for transfers between devices, swap(): return lax.ppermute(v, axis, [(i, i ^ bits) for i in range(n)])  51.7 us
    ppermute x26, starting transfers between devices, swap(): return lax.ppermute(v, axis, [(i, i ^ bits) for i in range(n)])  33.3 us
    ppermute x14, starting transfers between devices, shift(): return lax.ppermute(v, axis, [(i, (i + step) % n) for i in range(n)])  26.6 us
    ppermute x14, waiting for transfers between devices, shift(): return lax.ppermute(v, axis, [(i, (i + step) % n) for i in range(n)])  19.9 us
    pallas_call x2, Pallas kernels, late_product(): pl.pallas_call(kernel, out_shape=(one, one, two) * 2, in_specs=[VMEM] * (...  5.13 us
    pallas_call x1, Pallas kernels, early_product(): pl.pallas_call(kernel, out_shape=(jax.ShapeDtypeStruct((384, 1024), F32),...  3.43 us
  transfers between devices with their start and end apart: 40, of which 25 were waited for; matrix products, arithmetic and copies ran while one was open for 2% of the time, Pallas kernels for 5%

profile of v3, /device:TPU:8, one launch (start us, length us, event | category | flops | bytes accessed | tf_op | source)
XLA Modules:
  0.0 147.8 jit_solution(2327709574599911695)
XLA Ops:
  7.4 2.6 %collective-permute-start.2 = (f32[8,32,256]{2,1,0:T(8,128)S(1)}, f32[8,32,256]{2,1,0:T(8,128)S(1)}, u32[]{:S(2)}, u32[]{:S(2)}) collective-permute-start(f32[8,32,256]{2,1,0:T(8,128)S(1)} %get-tuple-element.57), channel_id=1, source_target_pairs={{0,192},{64,128},{128,64},{192,0},{1,193},{65,129},{129,65},{193,1... | collective-permute-start | bytes 786440 | tf_op jit(solution)/shard_map/ppermute | solution.py:21
  14.0 4.0 %collective-permute-start.13 = (f32[8,16,512]{2,1,0:T(8,128)S(1)}, f32[8,16,512]{2,1,0:T(8,128)S(1)}, u32[]{:S(2)}, u32[]{:S(2)}) collective-permute-start(f32[8,16,512]{2,1,0:T(8,128)S(1)} %get-tuple-element.37), channel_id=1, source_target_pairs={{0,28},{4,0},{8,4},{12,8},{16,12},{20,16},{24,20},{28,24},{1,29},{... | collective-permute-start | bytes 786440 | tf_op jit(solution)/shard_map/ppermute | solution.py:26
  18.1 3.3 %collective-permute-done.2 = f32[8,32,256]{2,1,0:T(8,128)S(1)} collective-permute-done((f32[8,32,256]{2,1,0:T(8,128)S(1)}, f32[8,32,256]{2,1,0:T(8,128)S(1)}, u32[]{:S(2)}, u32[]{:S(2)}) %collective-permute-start.2) | collective-permute-done | bytes 262176 | tf_op jit(solution)/shard_map/ppermute | solution.py:21
  23.2 3.9 %collective-permute-start.15 = (f32[8,16,512]{2,1,0:T(8,128)S(1)}, f32[8,16,512]{2,1,0:T(8,128)S(1)}, u32[]{:S(2)}, u32[]{:S(2)}) collective-permute-start(f32[8,16,512]{2,1,0:T(8,128)S(1)} %get-tuple-element.38), channel_id=1, source_target_pairs={{0,28},{4,0},{8,4},{12,8},{16,12},{20,16},{24,20},{28,24},{1,29},{... | collective-permute-start | bytes 786440 | tf_op jit(solution)/shard_map/ppermute | solution.py:26
  29.0 2.5 %collective-permute-done.15 = f32[8,16,512]{2,1,0:T(8,128)S(1)} collective-permute-done((f32[8,16,512]{2,1,0:T(8,128)S(1)}, f32[8,16,512]{2,1,0:T(8,128)S(1)}, u32[]{:S(2)}, u32[]{:S(2)}) %collective-permute-start.15) | collective-permute-done | bytes 262176 | tf_op jit(solution)/shard_map/ppermute | solution.py:26
  31.5 3.7 %collective-permute-start.19 = (f32[8,16,512]{2,1,0:T(8,128)S(1)}, f32[8,16,512]{2,1,0:T(8,128)S(1)}, u32[]{:S(2)}, u32[]{:S(2)}) collective-permute-start(f32[8,16,512]{2,1,0:T(8,128)S(1)} %collective-permute-done.15), channel_id=1, source_target_pairs={{0,28},{4,0},{8,4},{12,8},{16,12},{20,16},{24,20},{28,24},{1,29},{... | collective-permute-start | bytes 786440 | tf_op jit(solution)/shard_map/ppermute | solution.py:26
  39.0 5.3 %collective-permute-done.17 = f32[8,16,512]{2,1,0:T(8,128)S(1)} collective-permute-done((f32[8,16,512]{2,1,0:T(8,128)S(1)}, f32[8,16,512]{2,1,0:T(8,128)S(1)}, u32[]{:S(2)}, u32[]{:S(2)}) %collective-permute-start.17) | collective-permute-done | bytes 262176 | tf_op jit(solution)/shard_map/ppermute | solution.py:26
  44.3 3.7 %collective-permute-start.23 = (f32[8,16,512]{2,1,0:T(8,128)S(1)}, f32[8,16,512]{2,1,0:T(8,128)S(1)}, u32[]{:S(2)}, u32[]{:S(2)}) collective-permute-start(f32[8,16,512]{2,1,0:T(8,128)S(1)} %collective-permute-done.17), channel_id=1, source_target_pairs={{0,28},{4,0},{8,4},{12,8},{16,12},{20,16},{24,20},{28,24},{1,29},{... | collective-permute-start | bytes 786440 | tf_op jit(solution)/shard_map/ppermute | solution.py:26
  50.2 3.1 %collective-permute-done.23 = f32[8,16,512]{2,1,0:T(8,128)S(1)} collective-permute-done((f32[8,16,512]{2,1,0:T(8,128)S(1)}, f32[8,16,512]{2,1,0:T(8,128)S(1)}, u32[]{:S(2)}, u32[]{:S(2)}) %collective-permute-start.23) | collective-permute-done | bytes 262176 | tf_op jit(solution)/shard_map/ppermute | solution.py:26
  53.6 2.7 %collective-permute-done.25 = f32[8,16,512]{2,1,0:T(8,128)S(1)} collective-permute-done((f32[8,16,512]{2,1,0:T(8,128)S(1)}, f32[8,16,512]{2,1,0:T(8,128)S(1)}, u32[]{:S(2)}, u32[]{:S(2)}) %collective-permute-start.25) | collective-permute-done | bytes 262176 | tf_op jit(solution)/shard_map/ppermute | solution.py:26
  56.4 3.7 %collective-permute-start.27 = (f32[8,16,512]{2,1,0:T(8,128)S(1)}, f32[8,16,512]{2,1,0:T(8,128)S(1)}, u32[]{:S(2)}, u32[]{:S(2)}) collective-permute-start(f32[8,16,512]{2,1,0:T(8,128)S(1)} %collective-permute-done.25), channel_id=1, source_target_pairs={{0,28},{4,0},{8,4},{12,8},{16,12},{20,16},{24,20},{28,24},{1,29},{... | collective-permute-start | bytes 786440 | tf_op jit(solution)/shard_map/ppermute | solution.py:26
  60.1 3.5 %collective-permute-done.26 = f32[8,16,512]{2,1,0:T(8,128)S(1)} collective-permute-done((f32[8,16,512]{2,1,0:T(8,128)S(1)}, f32[8,16,512]{2,1,0:T(8,128)S(1)}, u32[]{:S(2)}, u32[]{:S(2)}) %collective-permute-start.26) | collective-permute-done | bytes 262176 | tf_op jit(solution)/shard_map/ppermute | solution.py:26
  68.3 6.5 %collective-permute-done.5 = f32[8,32,256]{2,1,0:T(8,128)S(1)} collective-permute-done((f32[8,32,256]{2,1,0:T(8,128)S(1)}, f32[8,32,256]{2,1,0:T(8,128)S(1)}, u32[]{:S(2)}, u32[]{:S(2)}) %collective-permute-start.5) | collective-permute-done | bytes 262176 | tf_op jit(solution)/shard_map/ppermute | solution.py:21
  75.8 8.8 %collective-permute-done.4.refs_3_ = f32[3,8,32,256]{3,2,1,0:T(8,128)S(1)} collective-permute-done((f32[3,8,32,256]{3,2,1,0:T(8,128)S(1)}, f32[3,8,32,256]{3,2,1,0:T(8,128)S(1)}, u32[]{:S(2)}, u32[]{:S(2)}) %collective-permute-start.4) | collective-permute-done | bytes 786464 | tf_op jit(solution)/shard_map/ppermute | solution.py:21
  86.3 3.8 %collective-permute-done.3 = f32[8,32,256]{2,1,0:T(8,128)S(1)} collective-permute-done((f32[8,32,256]{2,1,0:T(8,128)S(1)}, f32[8,32,256]{2,1,0:T(8,128)S(1)}, u32[]{:S(2)}, u32[]{:S(2)}) %collective-permute-start.3) | collective-permute-done | bytes 262176 | tf_op jit(solution)/shard_map/ppermute | solution.py:21
  93.7 7.2 %collective-permute-done.7.refs_0_ = f32[2,8,32,256]{3,2,1,0:T(8,128)S(1)} collective-permute-done((f32[2,8,32,256]{3,2,1,0:T(8,128)S(1)}, f32[2,8,32,256]{3,2,1,0:T(8,128)S(1)}, u32[]{:S(2)}, u32[]{:S(2)}) %collective-permute-start.7) | collective-permute-done | bytes 524320 | tf_op jit(solution)/shard_map/ppermute | solution.py:21
  100.9 3.0 %collective-permute-done.8.refs_1_ = f32[2,8,32,256]{3,2,1,0:T(8,128)S(1)} collective-permute-done((f32[2,8,32,256]{3,2,1,0:T(8,128)S(1)}, f32[2,8,32,256]{3,2,1,0:T(8,128)S(1)}, u32[]{:S(2)}, u32[]{:S(2)}) %collective-permute-start.8) | collective-permute-done | bytes 524320 | tf_op jit(solution)/shard_map/ppermute | solution.py:21
  104.3 3.4 %early_product.1 = (f32[384,1024]{1,0:T(8,128)S(1)}, bf16[3072,1024]{1,0:T(8,128)(2,1)S(1)}) custom-call(bf16[384,3072]{1,0:T(8,128)(2,1)S(1)} %get-tuple-element.32.a, f32[6,8,16,512]{3,2,1,0:T(8,128)S(1)} %bitcast_dynamic-update-slice_fusion.6.refs_0_, f32[4,8,16,512]{3,2,1,0:T(8,128)S(1)} %pad_maximum_fusion.refs_1_.refs_0_, ...), custom_call_target="tpu_custom_call" | custom-call | tf_op jit(solution)/shard_map/early_product/pallas_call | solution.py:183
  107.8 2.6 %late_product.3 = (f32[4,32,256]{2,1,0:T(8,128)S(1)}, f32[4,32,256]{2,1,0:T(8,128)S(1)}, f32[2,4,32,256]{3,2,1,0:T(8,128)S(1)}, f32[4,32,256]{2,1,0:T(8,128)S(1)...) custom-call(bf16[384,3072]{1,0:T(8,128)(2,1)S(1)} %get-tuple-element.29.a, ...), custom_call_target="tpu_custom_call" | custom-call | tf_op jit(solution)/shard_map/late_product/pallas_call | solution.py:225
  110.4 5.5 %collective-permute-start.35 = (f32[2,4,32,256]{3,2,1,0:T(8,128)S(1)}, f32[2,4,32,256]{3,2,1,0:T(8,128)S(1)}, u32[]{:S(2)}, u32[]{:S(2)}) collective-permute-start(f32[2,4,32,256]{3,2,1,0:T(8,128)S(1)} %get-tuple-element.51), channel_id=1, source_target_pairs={{0,192},{64,128},{128,64},{192,0},{1,193},{65,129},{129,65},{193,1... | collective-permute-start | bytes 786440 | tf_op jit(solution)/shard_map/ppermute | solution.py:21
  115.8 2.6 %late_product.2 = (f32[4,32,256]{2,1,0:T(8,128)S(1)}, f32[4,32,256]{2,1,0:T(8,128)S(1)}, f32[2,4,32,256]{3,2,1,0:T(8,128)S(1)}, f32[4,32,256]{2,1,0:T(8,128)S(1)...) custom-call(bf16[384,3072]{1,0:T(8,128)(2,1)S(1)} %get-tuple-element.29.a, ...), custom_call_target="tpu_custom_call" | custom-call | tf_op jit(solution)/shard_map/late_product/pallas_call | solution.py:225
  122.7 2.4 %collective-permute-done.33 = f32[2,4,32,256]{3,2,1,0:T(8,128)S(1)} collective-permute-done((f32[2,4,32,256]{3,2,1,0:T(8,128)S(1)}, f32[2,4,32,256]{3,2,1,0:T(8,128)S(1)}, u32[]{:S(2)}, u32[]{:S(2)}) %collective-permute-start.33) | collective-permute-done | bytes 262176 | tf_op jit(solution)/shard_map/ppermute | solution.py:21
  134.0 2.9 %collective-permute-done.30 = f32[4,32,256]{2,1,0:T(8,128)S(1)} collective-permute-done((f32[4,32,256]{2,1,0:T(8,128)S(1)}, f32[4,32,256]{2,1,0:T(8,128)S(1)}, u32[]{:S(2)}, u32[]{:S(2)}) %collective-permute-start.30) | collective-permute-done | bytes 131104 | tf_op jit(solution)/shard_map/ppermute | solution.py:21
  142.1 3.4 %collective-permute-done.38.refs_2_ = f32[32,1024]{1,0:T(8,128)S(1)} collective-permute-done((f32[32,1024]{1,0:T(8,128)S(1)}, f32[32,1024]{1,0:T(8,128)S(1)}, u32[]{:S(2)}, u32[]{:S(2)}) %collective-permute-start.38) | collective-permute-done | bytes 131104 | tf_op jit(solution)/shard_map/ppermute | solution.py:21
  (106 shorter events, 53.2 us)
Async XLA Ops:
  7.4 13.9 %collective-permute-start.2 = (f32[8,32,256]{2,1,0:T(8,128)S(1)}, f32[8,32,256]{2,1,0:T(8,128)S(1)}, u32[]{:S(2)}, u32[]{:S(2)}) collective-permute-start(f32[8,32,256]{2,1,0:T(8,128)S(1)} %get-tuple-element.57), channel_id=1, source_target_pairs={{0,192},{64,128},{128,64},{192,0},{1,193},{65,129},{129,65},{193,1... | collective-permute-start | bytes 786440 | tf_op jit(solution)/shard_map/ppermute | solution.py:21
  10.0 13.2 %collective-permute-start.1 = (f32[8,32,256]{2,1,0:T(8,128)S(1)}, f32[8,32,256]{2,1,0:T(8,128)S(1)}, u32[]{:S(2)}, u32[]{:S(2)}) collective-permute-start(f32[8,32,256]{2,1,0:T(8,128)S(1)} %get-tuple-element.54), channel_id=1, source_target_pairs={{0,128},{64,192},{128,0},{192,64},{1,129},{65,193},{129,1},{193,65... | collective-permute-start | bytes 786440 | tf_op jit(solution)/shard_map/ppermute | solution.py:21
  10.8 16.3 %collective-permute-start = (f32[8,32,256]{2,1,0:T(8,128)S(1)}, f32[8,32,256]{2,1,0:T(8,128)S(1)}, u32[]{:S(2)}, u32[]{:S(2)}) collective-permute-start(f32[8,32,256]{2,1,0:T(8,128)S(1)} %get-tuple-element.55), channel_id=1, source_target_pairs={{0,64},{64,0},{128,192},{192,128},{1,65},{65,1},{129,193},{193,129... | collective-permute-start | bytes 786440 | tf_op jit(solution)/shard_map/ppermute | solution.py:21
  12.0 16.9 %collective-permute-start.12 = (f32[8,16,512]{2,1,0:T(8,128)S(1)}, f32[8,16,512]{2,1,0:T(8,128)S(1)}, u32[]{:S(2)}, u32[]{:S(2)}) collective-permute-start(f32[8,16,512]{2,1,0:T(8,128)S(1)} %get-tuple-element.37), channel_id=1, source_target_pairs={{0,4},{4,8},{8,12},{12,16},{16,20},{20,24},{24,28},{28,0},{1,5},{5... | collective-permute-start | bytes 786440 | tf_op jit(solution)/shard_map/ppermute | solution.py:26
  14.0 21.2 %collective-permute-start.13 = (f32[8,16,512]{2,1,0:T(8,128)S(1)}, f32[8,16,512]{2,1,0:T(8,128)S(1)}, u32[]{:S(2)}, u32[]{:S(2)}) collective-permute-start(f32[8,16,512]{2,1,0:T(8,128)S(1)} %get-tuple-element.37), channel_id=1, source_target_pairs={{0,28},{4,0},{8,4},{12,8},{16,12},{20,16},{24,20},{28,24},{1,29},{... | collective-permute-start | bytes 786440 | tf_op jit(solution)/shard_map/ppermute | solution.py:26
  21.3 14.4 %collective-permute-start.14 = (f32[8,16,512]{2,1,0:T(8,128)S(1)}, f32[8,16,512]{2,1,0:T(8,128)S(1)}, u32[]{:S(2)}, u32[]{:S(2)}) collective-permute-start(f32[8,16,512]{2,1,0:T(8,128)S(1)} %get-tuple-element.38), channel_id=1, source_target_pairs={{0,4},{4,8},{8,12},{12,16},{16,20},{20,24},{24,28},{28,0},{1,5},{5... | collective-permute-start | bytes 786440 | tf_op jit(solution)/shard_map/ppermute | solution.py:26
  27.3 47.6 %collective-permute-start.6 = (f32[3,8,32,256]{3,2,1,0:T(8,128)S(1)}, f32[3,8,32,256]{3,2,1,0:T(8,128)S(1)}, u32[]{:S(2)}, u32[]{:S(2)}) collective-permute-start(f32[3,8,32,256]{3,2,1,0:T(8,128)S(1)} %pad_maximum_fusion.1.refs_1_), channel_id=1, source_target_pairs={{0,34},{2,32},{32,2},{34,0},{1,35},{3,33},{33,3},{35,1},{4,38},{6,... | collective-permute-start | bytes 2359304 | tf_op jit(solution)/shard_map/ppermute | solution.py:21
  28.9 10.0 %collective-permute-start.16 = (f32[8,16,512]{2,1,0:T(8,128)S(1)}, f32[8,16,512]{2,1,0:T(8,128)S(1)}, u32[]{:S(2)}, u32[]{:S(2)}) collective-permute-start(f32[8,16,512]{2,1,0:T(8,128)S(1)} %collective-permute-done.12), channel_id=1, source_target_pairs={{0,4},{4,8},{8,12},{12,16},{16,20},{20,24},{24,28},{28,0},{1,5},{5... | collective-permute-start | bytes 786440 | tf_op jit(solution)/shard_map/ppermute | solution.py:26
  31.5 16.5 %collective-permute-start.19 = (f32[8,16,512]{2,1,0:T(8,128)S(1)}, f32[8,16,512]{2,1,0:T(8,128)S(1)}, u32[]{:S(2)}, u32[]{:S(2)}) collective-permute-start(f32[8,16,512]{2,1,0:T(8,128)S(1)} %collective-permute-done.15), channel_id=1, source_target_pairs={{0,28},{4,0},{8,4},{12,8},{16,12},{20,16},{24,20},{28,24},{1,29},{... | collective-permute-start | bytes 786440 | tf_op jit(solution)/shard_map/ppermute | solution.py:26
  35.8 12.3 %collective-permute-start.18 = (f32[8,16,512]{2,1,0:T(8,128)S(1)}, f32[8,16,512]{2,1,0:T(8,128)S(1)}, u32[]{:S(2)}, u32[]{:S(2)}) collective-permute-start(f32[8,16,512]{2,1,0:T(8,128)S(1)} %collective-permute-done.14), channel_id=1, source_target_pairs={{0,4},{4,8},{8,12},{12,16},{16,20},{20,24},{24,28},{28,0},{1,5},{5... | collective-permute-start | bytes 786440 | tf_op jit(solution)/shard_map/ppermute | solution.py:26
  38.9 10.2 %collective-permute-start.22 = (f32[8,16,512]{2,1,0:T(8,128)S(1)}, f32[8,16,512]{2,1,0:T(8,128)S(1)}, u32[]{:S(2)}, u32[]{:S(2)}) collective-permute-start(f32[8,16,512]{2,1,0:T(8,128)S(1)} %collective-permute-done.16), channel_id=1, source_target_pairs={{0,4},{4,8},{8,12},{12,16},{16,20},{20,24},{24,28},{28,0},{1,5},{5... | collective-permute-start | bytes 786440 | tf_op jit(solution)/shard_map/ppermute | solution.py:26
  48.0 56.3 %collective-permute-start.20 = (f32[6,8,16,512]{3,2,1,0:T(8,128)S(1)}, f32[6,8,16,512]{3,2,1,0:T(8,128)S(1)}, u32[]{:S(2)}, u32[]{:S(2)}) collective-permute-start(f32[6,8,16,512]{3,2,1,0:T(8,128)S(1)} %bitcast_dynamic-update-slice_fusion.6.refs_0_), channel_id=1, source_target_pairs={{0,1},{1,0},{2,3},{3,2},{4,5},{5,4},{6,7},{7,6},{8,9},{9,8},{10,11... | collective-permute-start | bytes 4718600 | tf_op jit(solution)/shard_map/ppermute | solution.py:21
  49.1 11.0 %collective-permute-start.24 = (f32[8,16,512]{2,1,0:T(8,128)S(1)}, f32[8,16,512]{2,1,0:T(8,128)S(1)}, u32[]{:S(2)}, u32[]{:S(2)}) collective-permute-start(f32[8,16,512]{2,1,0:T(8,128)S(1)} %collective-permute-done.18), channel_id=1, source_target_pairs={{0,4},{4,8},{8,12},{12,16},{16,20},{20,24},{24,28},{28,0},{1,5},{5... | collective-permute-start | bytes 786440 | tf_op jit(solution)/shard_map/ppermute | solution.py:26
  53.4 10.3 %collective-permute-start.26 = (f32[8,16,512]{2,1,0:T(8,128)S(1)}, f32[8,16,512]{2,1,0:T(8,128)S(1)}, u32[]{:S(2)}, u32[]{:S(2)}) collective-permute-start(f32[8,16,512]{2,1,0:T(8,128)S(1)} %collective-permute-done.22), channel_id=1, source_target_pairs={{0,4},{4,8},{8,12},{12,16},{16,20},{20,24},{24,28},{28,0},{1,5},{5... | collective-permute-start | bytes 786440 | tf_op jit(solution)/shard_map/ppermute | solution.py:26
  64.0 43.8 %collective-permute-start.28 = (f32[6,8,16,512]{3,2,1,0:T(8,128)S(1)}, f32[6,8,16,512]{3,2,1,0:T(8,128)S(1)}, u32[]{:S(2)}, u32[]{:S(2)}) collective-permute-start(f32[6,8,16,512]{3,2,1,0:T(8,128)S(1)} %bitcast_dynamic-update-slice_fusion.refs_1_), channel_id=1, source_target_pairs={{0,1},{1,0},{2,3},{3,2},{4,5},{5,4},{6,7},{7,6},{8,9},{9,8},{10,11... | collective-permute-start | bytes 4718600 | tf_op jit(solution)/shard_map/ppermute | solution.py:21
  64.1 20.5 %collective-permute-start.4 = (f32[3,8,32,256]{3,2,1,0:T(8,128)S(1)}, f32[3,8,32,256]{3,2,1,0:T(8,128)S(1)}, u32[]{:S(2)}, u32[]{:S(2)}) collective-permute-start(f32[3,8,32,256]{3,2,1,0:T(8,128)S(1)} %pad_maximum_fusion.1.refs_1_), channel_id=1, source_target_pairs={{0,2},{2,0},{32,34},{34,32},{1,3},{3,1},{33,35},{35,33},{4,6},{6,4... | collective-permute-start | bytes 2359304 | tf_op jit(solution)/shard_map/ppermute | solution.py:21
  74.8 29.5 %collective-permute-start.21 = (f32[4,8,16,512]{3,2,1,0:T(8,128)S(1)}, f32[4,8,16,512]{3,2,1,0:T(8,128)S(1)}, u32[]{:S(2)}, u32[]{:S(2)}) collective-permute-start(f32[4,8,16,512]{3,2,1,0:T(8,128)S(1)} %pad_maximum_fusion.refs_1_.refs_0_), channel_id=1, source_target_pairs={{0,1},{1,0},{2,3},{3,2},{4,5},{5,4},{6,7},{7,6},{8,9},{9,8},{10,11... | collective-permute-start | bytes 3145736 | tf_op jit(solution)/shard_map/ppermute | solution.py:21
  74.8 15.4 %collective-permute-start.3 = (f32[8,32,256]{2,1,0:T(8,128)S(1)}, f32[8,32,256]{2,1,0:T(8,128)S(1)}, u32[]{:S(2)}, u32[]{:S(2)}) collective-permute-start(f32[8,32,256]{2,1,0:T(8,128)S(1)} %get-tuple-element.53), channel_id=1, source_target_pairs={{0,2},{2,0},{32,34},{34,32},{1,3},{3,1},{33,35},{35,33},{4,6},{6,4... | collective-permute-start | bytes 786440 | tf_op jit(solution)/shard_map/ppermute | solution.py:21
  84.6 16.3 %collective-permute-start.7 = (f32[2,8,32,256]{3,2,1,0:T(8,128)S(1)}, f32[2,8,32,256]{3,2,1,0:T(8,128)S(1)}, u32[]{:S(2)}, u32[]{:S(2)}) collective-permute-start(f32[2,8,32,256]{3,2,1,0:T(8,128)S(1)} %pad_maximum_fusion.2), channel_id=1, source_target_pairs={{0,2},{2,0},{32,34},{34,32},{1,3},{3,1},{33,35},{35,33},{4,6},{6,4... | collective-permute-start | bytes 1572872 | tf_op jit(solution)/shard_map/ppermute | solution.py:21
  90.2 13.7 %collective-permute-start.8 = (f32[2,8,32,256]{3,2,1,0:T(8,128)S(1)}, f32[2,8,32,256]{3,2,1,0:T(8,128)S(1)}, u32[]{:S(2)}, u32[]{:S(2)}) collective-permute-start(f32[2,8,32,256]{3,2,1,0:T(8,128)S(1)} %slice.57), channel_id=1, source_target_pairs={{0,34},{2,32},{32,2},{34,0},{1,35},{3,33},{33,3},{35,1},{4,38},{6,... | collective-permute-start | bytes 1572872 | tf_op jit(solution)/shard_map/ppermute | solution.py:21
  110.4 12.2 %collective-permute-start.35 = (f32[2,4,32,256]{3,2,1,0:T(8,128)S(1)}, f32[2,4,32,256]{3,2,1,0:T(8,128)S(1)}, u32[]{:S(2)}, u32[]{:S(2)}) collective-permute-start(f32[2,4,32,256]{3,2,1,0:T(8,128)S(1)} %get-tuple-element.51), channel_id=1, source_target_pairs={{0,192},{64,128},{128,64},{192,0},{1,193},{65,129},{129,65},{193,1... | collective-permute-start | bytes 786440 | tf_op jit(solution)/shard_map/ppermute | solution.py:21
  118.4 9.9 %collective-permute-start.31 = (f32[2,4,32,256]{3,2,1,0:T(8,128)S(1)}, f32[2,4,32,256]{3,2,1,0:T(8,128)S(1)}, u32[]{:S(2)}, u32[]{:S(2)}) collective-permute-start(f32[2,4,32,256]{3,2,1,0:T(8,128)S(1)} %get-tuple-element.45), channel_id=1, source_target_pairs={{0,192},{64,128},{128,64},{192,0},{1,193},{65,129},{129,65},{193,1... | collective-permute-start | bytes 786440 | tf_op jit(solution)/shard_map/ppermute | solution.py:21
  118.6 12.0 %collective-permute-start.29 = (f32[2,4,32,256]{3,2,1,0:T(8,128)S(1)}, f32[2,4,32,256]{3,2,1,0:T(8,128)S(1)}, u32[]{:S(2)}, u32[]{:S(2)}) collective-permute-start(f32[2,4,32,256]{3,2,1,0:T(8,128)S(1)} %get-tuple-element.42), channel_id=1, source_target_pairs={{0,64},{64,0},{128,192},{192,128},{1,65},{65,1},{129,193},{193,129... | collective-permute-start | bytes 786440 | tf_op jit(solution)/shard_map/ppermute | solution.py:21
  122.6 10.0 %collective-permute-start.36 = (f32[4,32,256]{2,1,0:T(8,128)S(1)}, f32[4,32,256]{2,1,0:T(8,128)S(1)}, u32[]{:S(2)}, u32[]{:S(2)}) collective-permute-start(f32[4,32,256]{2,1,0:T(8,128)S(1)} %fusion.42), channel_id=1, source_target_pairs={{0,64},{64,0},{128,192},{192,128},{1,65},{65,1},{129,193},{193,129... | collective-permute-start | bytes 393224 | tf_op jit(solution)/shard_map/ppermute | solution.py:21
  (18 other events, 128.0 us)

commit v4 on v3

--- a/solution.py
+++ b/solution.py
@@ -193,11 +193,25 @@
     )(left, *arrays)
 
 
+def far_product(left, right):
+    def kernel(a, b, o_ref):
+        o_ref[...] = product(a[...], b[...])
+
+    return pl.pallas_call(
+        kernel,
+        out_shape=jax.ShapeDtypeStruct((128, 1024), F32),
+        in_specs=[VMEM] * 2,
+        out_specs=VMEM,
+        compiler_params=PARAMS,
+        name="far_product",
+    )(left, right)
+
+
 def late_product(near, far, early, blocks, half):
     arrays, where = sources(blocks)
     n = len(arrays)
 
-    def kernel(a, far_early, far_late, total_ref, right_early, *refs):
+    def kernel(a, far_late, total_ref, far_ref, *refs):
         outs, right = refs[n : n + 6], refs[n + 6]
 
         def split(b, carry):
@@ -219,18 +233,18 @@
         near_total = product(a[...], right[...]) + total_ref[:, columns]
         for m, slot in enumerate((0, 1, 3)):
             put(slot, near_total[128 * m : 128 * m + 128])
-        put(2, product(far_early[...], right_early[:, columns]) + product(far_late[...], right[...]))
+        put(2, product(far_late[...], right[...]) + far_ref[:, columns])
 
     one, two = jax.ShapeDtypeStruct((4, 32, 256), F32), jax.ShapeDtypeStruct((2, 4, 32, 256), F32)
     return pl.pallas_call(
         kernel,
         out_shape=(one, one, two) * 2,
-        in_specs=[VMEM] * (n + 5),
+        in_specs=[VMEM] * (n + 4),
         out_specs=(VMEM,) * 6,
         scratch_shapes=[pltpu.VMEM((3072, 512), BF16)],
         compiler_params=PARAMS,
         name="late_product",
-    )(near[1], *far, *early, *arrays)
+    )(near, far, *early, *arrays)
 
 
 def placed_product(a, b):
@@ -271,6 +285,7 @@
     early = early_product(
         near[0], [[v[h][s] for v in (own, other) for s in EARLY] for h in range(2)]
     )
+    totals = early[0], far_product(far[0], early[1])
     held += [shift(up[0], "z", 1), shift(down[1], "z", -1)]
     places += [(0, 4), (1, 4)]
     both = jnp.stack(held)
@@ -281,7 +296,7 @@
     sums = []
     for h in range(2):
         blocks = [v[h][s] for v in (own, other) for s in LATE]
-        pieces = late_product(near, far, early, blocks, h)
+        pieces = late_product(near[1], far[1], totals, blocks, h)
         for quarter, (first, second) in enumerate(WAYS):
             keep, pass_on, send = pieces[3 * quarter : 3 * quarter + 3]
             got = swap(send, "x", first)

time: 150 us -> 151 us (level)
  transfers between devices with their start and end apart: 40 -> 40, of which waited for: 25 -> 25; matrix products, arithmetic and copies ran while one was open for 2% -> 2% of each run, Pallas kernels for 5% -> 6%
where the time goes in v4:
time: 151 us; the launch traced here: 148 us
  waiting for transfers between devices  72.3 us (48%)
  starting transfers between devices  59.7 us (40%)
  Pallas kernels  11.9 us (8%)
  local copies, waits for them, and re-layouts  2.25 us (1%)
    ppermute x26, waiting for transfers between devices, swap(): return lax.ppermute(v, axis, [(i, i ^ bits) for i in range(n)])  52.4 us
    ppermute x26, starting transfers between devices, swap(): return lax.ppermute(v, axis, [(i, i ^ bits) for i in range(n)])  33 us
    ppermute x14, starting transfers between devices, shift(): return lax.ppermute(v, axis, [(i, (i + step) % n) for i in range(n)])  26.6 us
    ppermute x14, waiting for transfers between devices, shift(): return lax.ppermute(v, axis, [(i, (i + step) % n) for i in range(n)])  19.9 us
    pallas_call x2, Pallas kernels, late_product(): pl.pallas_call(kernel, out_shape=(one, one, two) * 2, in_specs=[VMEM] * (...  4.33 us
    pallas_call x1, Pallas kernels, early_product(): pl.pallas_call(kernel, out_shape=(jax.ShapeDtypeStruct((384, 1024), F32),...  3.43 us
  transfers between devices with their start and end apart: 40, of which 25 were waited for; matrix products, arithmetic and copies ran while one was open for 2% of the time, Pallas kernels for 6%

profile of v4, /device:TPU:8, one launch (start us, length us, event | category | flops | bytes accessed | tf_op | source)
XLA Modules:
  0.0 148.4 jit_solution(16327978327128260880)
XLA Ops:
  7.4 2.6 %collective-permute-start.2 = (f32[8,32,256]{2,1,0:T(8,128)S(1)}, f32[8,32,256]{2,1,0:T(8,128)S(1)}, u32[]{:S(2)}, u32[]{:S(2)}) collective-permute-start(f32[8,32,256]{2,1,0:T(8,128)S(1)} %get-tuple-element.57), channel_id=1, source_target_pairs={{0,192},{64,128},{128,64},{192,0},{1,193},{65,129},{129,65},{193,1... | collective-permute-start | bytes 786440 | tf_op jit(solution)/shard_map/ppermute | solution.py:21
  14.0 4.0 %collective-permute-start.13 = (f32[8,16,512]{2,1,0:T(8,128)S(1)}, f32[8,16,512]{2,1,0:T(8,128)S(1)}, u32[]{:S(2)}, u32[]{:S(2)}) collective-permute-start(f32[8,16,512]{2,1,0:T(8,128)S(1)} %get-tuple-element.36), channel_id=1, source_target_pairs={{0,28},{4,0},{8,4},{12,8},{16,12},{20,16},{24,20},{28,24},{1,29},{... | collective-permute-start | bytes 786440 | tf_op jit(solution)/shard_map/ppermute | solution.py:26
  18.1 3.3 %collective-permute-done.2 = f32[8,32,256]{2,1,0:T(8,128)S(1)} collective-permute-done((f32[8,32,256]{2,1,0:T(8,128)S(1)}, f32[8,32,256]{2,1,0:T(8,128)S(1)}, u32[]{:S(2)}, u32[]{:S(2)}) %collective-permute-start.2) | collective-permute-done | bytes 262176 | tf_op jit(solution)/shard_map/ppermute | solution.py:21
  23.2 3.9 %collective-permute-start.15 = (f32[8,16,512]{2,1,0:T(8,128)S(1)}, f32[8,16,512]{2,1,0:T(8,128)S(1)}, u32[]{:S(2)}, u32[]{:S(2)}) collective-permute-start(f32[8,16,512]{2,1,0:T(8,128)S(1)} %get-tuple-element.37), channel_id=1, source_target_pairs={{0,28},{4,0},{8,4},{12,8},{16,12},{20,16},{24,20},{28,24},{1,29},{... | collective-permute-start | bytes 786440 | tf_op jit(solution)/shard_map/ppermute | solution.py:26
  29.0 2.5 %collective-permute-done.15 = f32[8,16,512]{2,1,0:T(8,128)S(1)} collective-permute-done((f32[8,16,512]{2,1,0:T(8,128)S(1)}, f32[8,16,512]{2,1,0:T(8,128)S(1)}, u32[]{:S(2)}, u32[]{:S(2)}) %collective-permute-start.15) | collective-permute-done | bytes 262176 | tf_op jit(solution)/shard_map/ppermute | solution.py:26
  31.5 3.7 %collective-permute-start.19 = (f32[8,16,512]{2,1,0:T(8,128)S(1)}, f32[8,16,512]{2,1,0:T(8,128)S(1)}, u32[]{:S(2)}, u32[]{:S(2)}) collective-permute-start(f32[8,16,512]{2,1,0:T(8,128)S(1)} %collective-permute-done.15), channel_id=1, source_target_pairs={{0,28},{4,0},{8,4},{12,8},{16,12},{20,16},{24,20},{28,24},{1,29},{... | collective-permute-start | bytes 786440 | tf_op jit(solution)/shard_map/ppermute | solution.py:26
  39.0 5.3 %collective-permute-done.17 = f32[8,16,512]{2,1,0:T(8,128)S(1)} collective-permute-done((f32[8,16,512]{2,1,0:T(8,128)S(1)}, f32[8,16,512]{2,1,0:T(8,128)S(1)}, u32[]{:S(2)}, u32[]{:S(2)}) %collective-permute-start.17) | collective-permute-done | bytes 262176 | tf_op jit(solution)/shard_map/ppermute | solution.py:26
  44.3 3.7 %collective-permute-start.23 = (f32[8,16,512]{2,1,0:T(8,128)S(1)}, f32[8,16,512]{2,1,0:T(8,128)S(1)}, u32[]{:S(2)}, u32[]{:S(2)}) collective-permute-start(f32[8,16,512]{2,1,0:T(8,128)S(1)} %collective-permute-done.17), channel_id=1, source_target_pairs={{0,28},{4,0},{8,4},{12,8},{16,12},{20,16},{24,20},{28,24},{1,29},{... | collective-permute-start | bytes 786440 | tf_op jit(solution)/shard_map/ppermute | solution.py:26
  50.2 3.1 %collective-permute-done.23 = f32[8,16,512]{2,1,0:T(8,128)S(1)} collective-permute-done((f32[8,16,512]{2,1,0:T(8,128)S(1)}, f32[8,16,512]{2,1,0:T(8,128)S(1)}, u32[]{:S(2)}, u32[]{:S(2)}) %collective-permute-start.23) | collective-permute-done | bytes 262176 | tf_op jit(solution)/shard_map/ppermute | solution.py:26
  53.6 2.7 %collective-permute-done.25 = f32[8,16,512]{2,1,0:T(8,128)S(1)} collective-permute-done((f32[8,16,512]{2,1,0:T(8,128)S(1)}, f32[8,16,512]{2,1,0:T(8,128)S(1)}, u32[]{:S(2)}, u32[]{:S(2)}) %collective-permute-start.25) | collective-permute-done | bytes 262176 | tf_op jit(solution)/shard_map/ppermute | solution.py:26
  56.4 3.7 %collective-permute-start.27 = (f32[8,16,512]{2,1,0:T(8,128)S(1)}, f32[8,16,512]{2,1,0:T(8,128)S(1)}, u32[]{:S(2)}, u32[]{:S(2)}) collective-permute-start(f32[8,16,512]{2,1,0:T(8,128)S(1)} %collective-permute-done.25), channel_id=1, source_target_pairs={{0,28},{4,0},{8,4},{12,8},{16,12},{20,16},{24,20},{28,24},{1,29},{... | collective-permute-start | bytes 786440 | tf_op jit(solution)/shard_map/ppermute | solution.py:26
  60.1 3.5 %collective-permute-done.26 = f32[8,16,512]{2,1,0:T(8,128)S(1)} collective-permute-done((f32[8,16,512]{2,1,0:T(8,128)S(1)}, f32[8,16,512]{2,1,0:T(8,128)S(1)}, u32[]{:S(2)}, u32[]{:S(2)}) %collective-permute-start.26) | collective-permute-done | bytes 262176 | tf_op jit(solution)/shard_map/ppermute | solution.py:26
  65.9 2.3 %collective-permute-start.5 = (f32[8,32,256]{2,1,0:T(8,128)S(1)}, f32[8,32,256]{2,1,0:T(8,128)S(1)}, u32[]{:S(2)}, u32[]{:S(2)}) collective-permute-start(f32[8,32,256]{2,1,0:T(8,128)S(1)} %get-tuple-element.53), channel_id=1, source_target_pairs={{0,34},{2,32},{32,2},{34,0},{1,35},{3,33},{33,3},{35,1},{4,38},{6,... | collective-permute-start | bytes 786440 | tf_op jit(solution)/shard_map/ppermute | solution.py:21
  68.3 6.5 %collective-permute-done.5 = f32[8,32,256]{2,1,0:T(8,128)S(1)} collective-permute-done((f32[8,32,256]{2,1,0:T(8,128)S(1)}, f32[8,32,256]{2,1,0:T(8,128)S(1)}, u32[]{:S(2)}, u32[]{:S(2)}) %collective-permute-start.5) | collective-permute-done | bytes 262176 | tf_op jit(solution)/shard_map/ppermute | solution.py:21
  75.8 8.8 %collective-permute-done.4.refs_3_ = f32[3,8,32,256]{3,2,1,0:T(8,128)S(1)} collective-permute-done((f32[3,8,32,256]{3,2,1,0:T(8,128)S(1)}, f32[3,8,32,256]{3,2,1,0:T(8,128)S(1)}, u32[]{:S(2)}, u32[]{:S(2)}) %collective-permute-start.4) | collective-permute-done | bytes 786464 | tf_op jit(solution)/shard_map/ppermute | solution.py:21
  86.3 3.8 %collective-permute-done.3 = f32[8,32,256]{2,1,0:T(8,128)S(1)} collective-permute-done((f32[8,32,256]{2,1,0:T(8,128)S(1)}, f32[8,32,256]{2,1,0:T(8,128)S(1)}, u32[]{:S(2)}, u32[]{:S(2)}) %collective-permute-start.3) | collective-permute-done | bytes 262176 | tf_op jit(solution)/shard_map/ppermute | solution.py:21
  93.7 7.2 %collective-permute-done.7.refs_0_ = f32[2,8,32,256]{3,2,1,0:T(8,128)S(1)} collective-permute-done((f32[2,8,32,256]{3,2,1,0:T(8,128)S(1)}, f32[2,8,32,256]{3,2,1,0:T(8,128)S(1)}, u32[]{:S(2)}, u32[]{:S(2)}) %collective-permute-start.7) | collective-permute-done | bytes 524320 | tf_op jit(solution)/shard_map/ppermute | solution.py:21
  100.9 3.0 %collective-permute-done.8.refs_1_ = f32[2,8,32,256]{3,2,1,0:T(8,128)S(1)} collective-permute-done((f32[2,8,32,256]{3,2,1,0:T(8,128)S(1)}, f32[2,8,32,256]{3,2,1,0:T(8,128)S(1)}, u32[]{:S(2)}, u32[]{:S(2)}) %collective-permute-start.8) | collective-permute-done | bytes 524320 | tf_op jit(solution)/shard_map/ppermute | solution.py:21
  104.3 3.4 %early_product.1 = (f32[384,1024]{1,0:T(8,128)S(1)}, bf16[3072,1024]{1,0:T(8,128)(2,1)S(1)}) custom-call(bf16[384,3072]{1,0:T(8,128)(2,1)S(1)} %get-tuple-element.31.a, f32[6,8,16,512]{3,2,1,0:T(8,128)S(1)} %bitcast_dynamic-update-slice_fusion.6.refs_0_, f32[4,8,16,512]{3,2,1,0:T(8,128)S(1)} %pad_maximum_fusion.refs_1_.refs_0_, ...), custom_call_target="tpu_custom_call" | custom-call | tf_op jit(solution)/shard_map/early_product/pallas_call | solution.py:183
  111.0 5.5 %collective-permute-start.35 = (f32[2,4,32,256]{3,2,1,0:T(8,128)S(1)}, f32[2,4,32,256]{3,2,1,0:T(8,128)S(1)}, u32[]{:S(2)}, u32[]{:S(2)}) collective-permute-start(f32[2,4,32,256]{3,2,1,0:T(8,128)S(1)} %get-tuple-element.51), channel_id=1, source_target_pairs={{0,192},{64,128},{128,64},{192,0},{1,193},{65,129},{129,65},{193,1... | collective-permute-start | bytes 786440 | tf_op jit(solution)/shard_map/ppermute | solution.py:21
  120.8 2.3 %collective-permute-done.35 = f32[2,4,32,256]{3,2,1,0:T(8,128)S(1)} collective-permute-done((f32[2,4,32,256]{3,2,1,0:T(8,128)S(1)}, f32[2,4,32,256]{3,2,1,0:T(8,128)S(1)}, u32[]{:S(2)}, u32[]{:S(2)}) %collective-permute-start.35) | collective-permute-done | bytes 262176 | tf_op jit(solution)/shard_map/ppermute | solution.py:21
  123.2 2.4 %collective-permute-done.33 = f32[2,4,32,256]{3,2,1,0:T(8,128)S(1)} collective-permute-done((f32[2,4,32,256]{3,2,1,0:T(8,128)S(1)}, f32[2,4,32,256]{3,2,1,0:T(8,128)S(1)}, u32[]{:S(2)}, u32[]{:S(2)}) %collective-permute-start.33) | collective-permute-done | bytes 262176 | tf_op jit(solution)/shard_map/ppermute | solution.py:21
  134.6 2.9 %collective-permute-done.30 = f32[4,32,256]{2,1,0:T(8,128)S(1)} collective-permute-done((f32[4,32,256]{2,1,0:T(8,128)S(1)}, f32[4,32,256]{2,1,0:T(8,128)S(1)}, u32[]{:S(2)}, u32[]{:S(2)}) %collective-permute-start.30) | collective-permute-done | bytes 131104 | tf_op jit(solution)/shard_map/ppermute | solution.py:21
  142.7 3.4 %collective-permute-done.38.refs_2_ = f32[32,1024]{1,0:T(8,128)S(1)} collective-permute-done((f32[32,1024]{1,0:T(8,128)S(1)}, f32[32,1024]{1,0:T(8,128)S(1)}, u32[]{:S(2)}, u32[]{:S(2)}) %collective-permute-start.38) | collective-permute-done | bytes 131104 | tf_op jit(solution)/shard_map/ppermute | solution.py:21
  (107 shorter events, 54.3 us)
Async XLA Ops:
  7.4 13.9 %collective-permute-start.2 = (f32[8,32,256]{2,1,0:T(8,128)S(1)}, f32[8,32,256]{2,1,0:T(8,128)S(1)}, u32[]{:S(2)}, u32[]{:S(2)}) collective-permute-start(f32[8,32,256]{2,1,0:T(8,128)S(1)} %get-tuple-element.57), channel_id=1, source_target_pairs={{0,192},{64,128},{128,64},{192,0},{1,193},{65,129},{129,65},{193,1... | collective-permute-start | bytes 786440 | tf_op jit(solution)/shard_map/ppermute | solution.py:21
  10.0 13.2 %collective-permute-start.1 = (f32[8,32,256]{2,1,0:T(8,128)S(1)}, f32[8,32,256]{2,1,0:T(8,128)S(1)}, u32[]{:S(2)}, u32[]{:S(2)}) collective-permute-start(f32[8,32,256]{2,1,0:T(8,128)S(1)} %get-tuple-element.54), channel_id=1, source_target_pairs={{0,128},{64,192},{128,0},{192,64},{1,129},{65,193},{129,1},{193,65... | collective-permute-start | bytes 786440 | tf_op jit(solution)/shard_map/ppermute | solution.py:21
  10.8 16.3 %collective-permute-start = (f32[8,32,256]{2,1,0:T(8,128)S(1)}, f32[8,32,256]{2,1,0:T(8,128)S(1)}, u32[]{:S(2)}, u32[]{:S(2)}) collective-permute-start(f32[8,32,256]{2,1,0:T(8,128)S(1)} %get-tuple-element.55), channel_id=1, source_target_pairs={{0,64},{64,0},{128,192},{192,128},{1,65},{65,1},{129,193},{193,129... | collective-permute-start | bytes 786440 | tf_op jit(solution)/shard_map/ppermute | solution.py:21
  12.0 16.9 %collective-permute-start.12 = (f32[8,16,512]{2,1,0:T(8,128)S(1)}, f32[8,16,512]{2,1,0:T(8,128)S(1)}, u32[]{:S(2)}, u32[]{:S(2)}) collective-permute-start(f32[8,16,512]{2,1,0:T(8,128)S(1)} %get-tuple-element.36), channel_id=1, source_target_pairs={{0,4},{4,8},{8,12},{12,16},{16,20},{20,24},{24,28},{28,0},{1,5},{5... | collective-permute-start | bytes 786440 | tf_op jit(solution)/shard_map/ppermute | solution.py:26
  14.0 21.2 %collective-permute-start.13 = (f32[8,16,512]{2,1,0:T(8,128)S(1)}, f32[8,16,512]{2,1,0:T(8,128)S(1)}, u32[]{:S(2)}, u32[]{:S(2)}) collective-permute-start(f32[8,16,512]{2,1,0:T(8,128)S(1)} %get-tuple-element.36), channel_id=1, source_target_pairs={{0,28},{4,0},{8,4},{12,8},{16,12},{20,16},{24,20},{28,24},{1,29},{... | collective-permute-start | bytes 786440 | tf_op jit(solution)/shard_map/ppermute | solution.py:26
  21.3 14.4 %collective-permute-start.14 = (f32[8,16,512]{2,1,0:T(8,128)S(1)}, f32[8,16,512]{2,1,0:T(8,128)S(1)}, u32[]{:S(2)}, u32[]{:S(2)}) collective-permute-start(f32[8,16,512]{2,1,0:T(8,128)S(1)} %get-tuple-element.37), channel_id=1, source_target_pairs={{0,4},{4,8},{8,12},{12,16},{16,20},{20,24},{24,28},{28,0},{1,5},{5... | collective-permute-start | bytes 786440 | tf_op jit(solution)/shard_map/ppermute | solution.py:26
  27.3 47.6 %collective-permute-start.6 = (f32[3,8,32,256]{3,2,1,0:T(8,128)S(1)}, f32[3,8,32,256]{3,2,1,0:T(8,128)S(1)}, u32[]{:S(2)}, u32[]{:S(2)}) collective-permute-start(f32[3,8,32,256]{3,2,1,0:T(8,128)S(1)} %pad_maximum_fusion.1.refs_1_), channel_id=1, source_target_pairs={{0,34},{2,32},{32,2},{34,0},{1,35},{3,33},{33,3},{35,1},{4,38},{6,... | collective-permute-start | bytes 2359304 | tf_op jit(solution)/shard_map/ppermute | solution.py:21
  28.9 10.0 %collective-permute-start.16 = (f32[8,16,512]{2,1,0:T(8,128)S(1)}, f32[8,16,512]{2,1,0:T(8,128)S(1)}, u32[]{:S(2)}, u32[]{:S(2)}) collective-permute-start(f32[8,16,512]{2,1,0:T(8,128)S(1)} %collective-permute-done.12), channel_id=1, source_target_pairs={{0,4},{4,8},{8,12},{12,16},{16,20},{20,24},{24,28},{28,0},{1,5},{5... | collective-permute-start | bytes 786440 | tf_op jit(solution)/shard_map/ppermute | solution.py:26
  31.5 16.5 %collective-permute-start.19 = (f32[8,16,512]{2,1,0:T(8,128)S(1)}, f32[8,16,512]{2,1,0:T(8,128)S(1)}, u32[]{:S(2)}, u32[]{:S(2)}) collective-permute-start(f32[8,16,512]{2,1,0:T(8,128)S(1)} %collective-permute-done.15), channel_id=1, source_target_pairs={{0,28},{4,0},{8,4},{12,8},{16,12},{20,16},{24,20},{28,24},{1,29},{... | collective-permute-start | bytes 786440 | tf_op jit(solution)/shard_map/ppermute | solution.py:26
  35.8 12.3 %collective-permute-start.18 = (f32[8,16,512]{2,1,0:T(8,128)S(1)}, f32[8,16,512]{2,1,0:T(8,128)S(1)}, u32[]{:S(2)}, u32[]{:S(2)}) collective-permute-start(f32[8,16,512]{2,1,0:T(8,128)S(1)} %collective-permute-done.14), channel_id=1, source_target_pairs={{0,4},{4,8},{8,12},{12,16},{16,20},{20,24},{24,28},{28,0},{1,5},{5... | collective-permute-start | bytes 786440 | tf_op jit(solution)/shard_map/ppermute | solution.py:26
  38.9 10.2 %collective-permute-start.22 = (f32[8,16,512]{2,1,0:T(8,128)S(1)}, f32[8,16,512]{2,1,0:T(8,128)S(1)}, u32[]{:S(2)}, u32[]{:S(2)}) collective-permute-start(f32[8,16,512]{2,1,0:T(8,128)S(1)} %collective-permute-done.16), channel_id=1, source_target_pairs={{0,4},{4,8},{8,12},{12,16},{16,20},{20,24},{24,28},{28,0},{1,5},{5... | collective-permute-start | bytes 786440 | tf_op jit(solution)/shard_map/ppermute | solution.py:26
  48.0 56.3 %collective-permute-start.20 = (f32[6,8,16,512]{3,2,1,0:T(8,128)S(1)}, f32[6,8,16,512]{3,2,1,0:T(8,128)S(1)}, u32[]{:S(2)}, u32[]{:S(2)}) collective-permute-start(f32[6,8,16,512]{3,2,1,0:T(8,128)S(1)} %bitcast_dynamic-update-slice_fusion.6.refs_0_), channel_id=1, source_target_pairs={{0,1},{1,0},{2,3},{3,2},{4,5},{5,4},{6,7},{7,6},{8,9},{9,8},{10,11... | collective-permute-start | bytes 4718600 | tf_op jit(solution)/shard_map/ppermute | solution.py:21
  49.1 11.0 %collective-permute-start.24 = (f32[8,16,512]{2,1,0:T(8,128)S(1)}, f32[8,16,512]{2,1,0:T(8,128)S(1)}, u32[]{:S(2)}, u32[]{:S(2)}) collective-permute-start(f32[8,16,512]{2,1,0:T(8,128)S(1)} %collective-permute-done.18), channel_id=1, source_target_pairs={{0,4},{4,8},{8,12},{12,16},{16,20},{20,24},{24,28},{28,0},{1,5},{5... | collective-permute-start | bytes 786440 | tf_op jit(solution)/shard_map/ppermute | solution.py:26
  53.4 10.3 %collective-permute-start.26 = (f32[8,16,512]{2,1,0:T(8,128)S(1)}, f32[8,16,512]{2,1,0:T(8,128)S(1)}, u32[]{:S(2)}, u32[]{:S(2)}) collective-permute-start(f32[8,16,512]{2,1,0:T(8,128)S(1)} %collective-permute-done.22), channel_id=1, source_target_pairs={{0,4},{4,8},{8,12},{12,16},{16,20},{20,24},{24,28},{28,0},{1,5},{5... | collective-permute-start | bytes 786440 | tf_op jit(solution)/shard_map/ppermute | solution.py:26
  64.0 44.8 %collective-permute-start.28 = (f32[6,8,16,512]{3,2,1,0:T(8,128)S(1)}, f32[6,8,16,512]{3,2,1,0:T(8,128)S(1)}, u32[]{:S(2)}, u32[]{:S(2)}) collective-permute-start(f32[6,8,16,512]{3,2,1,0:T(8,128)S(1)} %bitcast_dynamic-update-slice_fusion.refs_1_), channel_id=1, source_target_pairs={{0,1},{1,0},{2,3},{3,2},{4,5},{5,4},{6,7},{7,6},{8,9},{9,8},{10,11... | collective-permute-start | bytes 4718600 | tf_op jit(solution)/shard_map/ppermute | solution.py:21
  64.1 20.5 %collective-permute-start.4 = (f32[3,8,32,256]{3,2,1,0:T(8,128)S(1)}, f32[3,8,32,256]{3,2,1,0:T(8,128)S(1)}, u32[]{:S(2)}, u32[]{:S(2)}) collective-permute-start(f32[3,8,32,256]{3,2,1,0:T(8,128)S(1)} %pad_maximum_fusion.1.refs_1_), channel_id=1, source_target_pairs={{0,2},{2,0},{32,34},{34,32},{1,3},{3,1},{33,35},{35,33},{4,6},{6,4... | collective-permute-start | bytes 2359304 | tf_op jit(solution)/shard_map/ppermute | solution.py:21
  74.8 29.5 %collective-permute-start.21 = (f32[4,8,16,512]{3,2,1,0:T(8,128)S(1)}, f32[4,8,16,512]{3,2,1,0:T(8,128)S(1)}, u32[]{:S(2)}, u32[]{:S(2)}) collective-permute-start(f32[4,8,16,512]{3,2,1,0:T(8,128)S(1)} %pad_maximum_fusion.refs_1_.refs_0_), channel_id=1, source_target_pairs={{0,1},{1,0},{2,3},{3,2},{4,5},{5,4},{6,7},{7,6},{8,9},{9,8},{10,11... | collective-permute-start | bytes 3145736 | tf_op jit(solution)/shard_map/ppermute | solution.py:21
  74.8 15.4 %collective-permute-start.3 = (f32[8,32,256]{2,1,0:T(8,128)S(1)}, f32[8,32,256]{2,1,0:T(8,128)S(1)}, u32[]{:S(2)}, u32[]{:S(2)}) collective-permute-start(f32[8,32,256]{2,1,0:T(8,128)S(1)} %get-tuple-element.53), channel_id=1, source_target_pairs={{0,2},{2,0},{32,34},{34,32},{1,3},{3,1},{33,35},{35,33},{4,6},{6,4... | collective-permute-start | bytes 786440 | tf_op jit(solution)/shard_map/ppermute | solution.py:21
  84.6 16.3 %collective-permute-start.7 = (f32[2,8,32,256]{3,2,1,0:T(8,128)S(1)}, f32[2,8,32,256]{3,2,1,0:T(8,128)S(1)}, u32[]{:S(2)}, u32[]{:S(2)}) collective-permute-start(f32[2,8,32,256]{3,2,1,0:T(8,128)S(1)} %pad_maximum_fusion.2), channel_id=1, source_target_pairs={{0,2},{2,0},{32,34},{34,32},{1,3},{3,1},{33,35},{35,33},{4,6},{6,4... | collective-permute-start | bytes 1572872 | tf_op jit(solution)/shard_map/ppermute | solution.py:21
  90.2 13.7 %collective-permute-start.8 = (f32[2,8,32,256]{3,2,1,0:T(8,128)S(1)}, f32[2,8,32,256]{3,2,1,0:T(8,128)S(1)}, u32[]{:S(2)}, u32[]{:S(2)}) collective-permute-start(f32[2,8,32,256]{3,2,1,0:T(8,128)S(1)} %slice.57), channel_id=1, source_target_pairs={{0,34},{2,32},{32,2},{34,0},{1,35},{3,33},{33,3},{35,1},{4,38},{6,... | collective-permute-start | bytes 1572872 | tf_op jit(solution)/shard_map/ppermute | solution.py:21
  111.0 12.2 %collective-permute-start.35 = (f32[2,4,32,256]{3,2,1,0:T(8,128)S(1)}, f32[2,4,32,256]{3,2,1,0:T(8,128)S(1)}, u32[]{:S(2)}, u32[]{:S(2)}) collective-permute-start(f32[2,4,32,256]{3,2,1,0:T(8,128)S(1)} %get-tuple-element.51), channel_id=1, source_target_pairs={{0,192},{64,128},{128,64},{192,0},{1,193},{65,129},{129,65},{193,1... | collective-permute-start | bytes 786440 | tf_op jit(solution)/shard_map/ppermute | solution.py:21
  118.6 10.3 %collective-permute-start.31 = (f32[2,4,32,256]{3,2,1,0:T(8,128)S(1)}, f32[2,4,32,256]{3,2,1,0:T(8,128)S(1)}, u32[]{:S(2)}, u32[]{:S(2)}) collective-permute-start(f32[2,4,32,256]{3,2,1,0:T(8,128)S(1)} %get-tuple-element.45), channel_id=1, source_target_pairs={{0,192},{64,128},{128,64},{192,0},{1,193},{65,129},{129,65},{193,1... | collective-permute-start | bytes 786440 | tf_op jit(solution)/shard_map/ppermute | solution.py:21
  118.8 12.4 %collective-permute-start.29 = (f32[2,4,32,256]{3,2,1,0:T(8,128)S(1)}, f32[2,4,32,256]{3,2,1,0:T(8,128)S(1)}, u32[]{:S(2)}, u32[]{:S(2)}) collective-permute-start(f32[2,4,32,256]{3,2,1,0:T(8,128)S(1)} %get-tuple-element.42), channel_id=1, source_target_pairs={{0,64},{64,0},{128,192},{192,128},{1,65},{65,1},{129,193},{193,129... | collective-permute-start | bytes 786440 | tf_op jit(solution)/shard_map/ppermute | solution.py:21
  123.1 10.0 %collective-permute-start.36 = (f32[4,32,256]{2,1,0:T(8,128)S(1)}, f32[4,32,256]{2,1,0:T(8,128)S(1)}, u32[]{:S(2)}, u32[]{:S(2)}) collective-permute-start(f32[4,32,256]{2,1,0:T(8,128)S(1)} %fusion.42), channel_id=1, source_target_pairs={{0,64},{64,0},{128,192},{192,128},{1,65},{65,1},{129,193},{193,129... | collective-permute-start | bytes 393224 | tf_op jit(solution)/shard_map/ppermute | solution.py:21
  (18 other events, 128.0 us)
